TPU v7x, 256 devices: a whole 4x4x8 slice. The times are simulated.
256 devices in a mesh: dp: 4 (over y), ctx: 64 (over x, z, core).
Axes of the slice: x: 4, y: 4, z: 8, core: 2. Of those that a mesh axis runs over, the one named last changes fastest.
Arguments:
- hidden: bfloat16 [4, 32768, 8192], P('dp', 'ctx'), may hold values from -8 to 8
- norm_gain: float32 [8192], replicated, may hold values from 0.3 to 5.2
- cotangent: bfloat16 [4, 32768, 512], P('dp', 'ctx'), may hold values from -30 to 30
- loss_weight: float32 [4], P('dp'), may hold values from 0.08 to 5
Outputs:
- clipped_grad: float32 [8192, 512], P('ctx', 'dp')
All inputs are finite; a program needn't handle non-finite values.
Results may differ from a plain program's by a relative error of at most 0.0022.
Values may be sent and summed in bfloat16 or wider, within the bound.
No kernel may reach another device: no remote copies, remote signals or barrier semaphores. Data moves between devices by JAX's collectives and lax.ppermute only.
A program may use at most 64 MiB of HBM per device.

v0:
```python
import math

import jax
import jax.numpy as jnp
from jax import lax
from jax.sharding import PartitionSpec as P


def sent_to_all(value, axis):
    copies = jnp.broadcast_to(value, (lax.axis_size(axis), *value.shape))
    return lax.all_to_all(copies, axis, split_axis=0, concat_axis=0, tiled=True)


def taken_together(value, axis):
    return sent_to_all(value, axis).sum(axis=0)


def in_blocks(value, dim, peers):
    dims = value.shape
    parts = value.reshape(*dims[:dim], peers, dims[dim] // peers, *dims[dim + 1 :])
    return jnp.moveaxis(parts, dim, 0)


def summed_on_arrival(value, axis, dim):
    parts = in_blocks(value, dim, lax.axis_size(axis))
    arrived = lax.all_to_all(parts, axis, split_axis=0, concat_axis=0, tiled=True)
    return arrived.sum(axis=0)


def per_device(hidden, norm_gain, cotangent, loss_weight):
    widened = hidden[0].astype(jnp.float32)
    scale = lax.rsqrt(jnp.mean(widened * widened, axis=1, keepdims=True) + 1e-05)
    normed = (widened * scale * norm_gain).astype(jnp.bfloat16)
    upstream = cotangent[0]
    context_size = lax.axis_size("ctx")
    doc_length = upstream.shape[0] * context_size
    weight = loss_weight[0] / math.sqrt(doc_length)
    features = normed.shape[1]
    outputs = upstream.shape[1]
    contract = (((0,), (0,)), ((), ()))
    owned_tile = lax.psum_scatter(
        weight * lax.dot_general(normed, upstream, contract, preferred_element_type=jnp.float32),
        "ctx",
        scatter_dimension=0,
        tiled=True,
    )
    squares = jnp.sum(owned_tile * owned_tile)
    clip_bound = math.sqrt(features * outputs)
    summed = taken_together(squares, "ctx")
    factor = jnp.minimum(1.0, clip_bound * lax.rsqrt(summed + 1e-06))
    result = summed_on_arrival(factor * owned_tile, "dp", 1)
    return result


def solution(mesh):
    in_specs = (P("dp", "ctx", None), P(), P("dp", "ctx", None), P("dp"))
    out_specs = P("ctx", "dp")
    return jax.shard_map(
        per_device, mesh=mesh, in_specs=in_specs, out_specs=out_specs, check_vma=False
    )
```

profile of v0, /device:TPU:1, one launch (start us, length us, event | category | flops | bytes accessed | tf_op | source)
XLA Modules:
  0.0 257.4 jit_solution(3803205726008628977)
XLA Ops:
  6.5 0.0 copy-start
  6.5 0.0 reduce-scatter.2.cloned.1.call-start
  7.2 5.1 %fusion = f32[512]{0:T(512)S(1)} fusion(bf16[1,512,8192]{2,1,0:T(8,128)(2,1)} %param.4), kind=kLoop, calls=%fused_computation.2 | loop fusion | flops 12582400 | bytes 8390656 | tf_op jit(solution)/shard_map/reduce_sum | solution.py:32
  12.4 0.0 copy-done
  12.4 13.0 %convolution_multiply_fusion = f32[8192,512]{1,0:T(8,128)} fusion(bf16[1,512,8192]{2,1,0:T(8,128)(2,1)} %param.4, f32[8192]{0:T(1024)} %param.5, f32[512]{0:T(512)S(1)} %add_rsqrt_fusion, f32[]{:T(128)} %bitcast, bf16[1,512,512]{2,1,0:T(8,128)(2,1)S(1)} %copy-done), kind=kOutput, calls=%fused_computation.5 | convolution fusion | flops 4315938816 | bytes 25724932 | tf_op jit(solution)/shard_map/dot_general | solution.py:42
  25.4 0.0 reduce-scatter.2.cloned.1.call-update
  25.4 189.6 %reduce-scatter.2.cloned.1.call-done = f32[128,512]{1,0:T(8,128)} async-done(((f32[8192,512]{1,0:T(8,128)}), f32[128,512]{1,0:T(8,128)}) %reduce-scatter.2.cloned.1.call-update) | async-done | bytes 262160 | tf_op jit(solution)/shard_map/reduce_scatter | solution.py:41
  215.0 1.6 multiply_reduce_fusion
  216.7 0.7 broadcast_in_dim.2
  217.3 21.0 %all_to_all.11 = f32[64,1,1]{2,1,0:T(1,128)S(1)} all-to-all(f32[64,1,1]{2,1,0:T(1,128)S(1)} %broadcast_in_dim.2), channel_id=1, replica_groups=mesh['dp'=4,'ctx'=64] {'ctx'}, dimensions={0} | all-to-all | bytes 512 | tf_op jit(solution)/shard_map/all_to_all | solution.py:11
  238.3 0.7 reduce_sum.38
  239.7 1.0 bitcast_bitcast_fusion
  240.6 9.3 %all_to_all.12 = f32[4,128,128]{2,1,0:T(8,128)S(1)} all-to-all(f32[4,128,128]{2,1,0:T(8,128)S(1)} %bitcast_bitcast_fusion), channel_id=1, replica_groups=mesh['dp'=4,'ctx'=64] {'dp'}, dimensions={0} | all-to-all | bytes 524288 | tf_op jit(solution)/shard_map/all_to_all | solution.py:26
  250.0 0.6 reduce_sum.39
  (1 shorter events, 0.0 us)
Async XLA Ops:
  6.5 5.8 %copy-start = (bf16[1,512,512]{2,1,0:T(8,128)(2,1)S(1)}, bf16[1,512,512]{2,1,0:T(8,128)(2,1)}, u32[]{:S(2)}) copy-start(bf16[1,512,512]{2,1,0:T(8,128)(2,1)} %param.6) | copy-start | bytes 1572868
  6.5 208.5 %reduce-scatter.2.cloned.1.call-start = ((), (), s32[]{:S(2)}) async-start(), calls=%async_computation.3 | async-start | bytes 17039360 | tf_op jit(solution)/shard_map/reduce_scatter | solution.py:41
Sparse Core Ops, SparseCore 0:
  25.5 189.4 reduce-scatter.1
where the time goes:
time: 258 us; the launch traced here: 257 us
  waiting for transfers between devices  190 us (74%)
  blocking collectives  30.3 us (12%)
  between operations  14.8 us (6%)
  matrix products  13 us (5%)
  other arithmetic  9.02 us (3%)
    reduce_scatter x1, waiting for transfers between devices, per_device(): lax.psum_scatter(weight * lax.dot_general(normed, upstream, contract, pre...  190 us
    all_to_all x1, blocking collectives, sent_to_all(): return lax.all_to_all(copies, axis, split_axis=0, concat_axis=0, tiled=True)  21 us
    dot_general x1, matrix products, per_device(): lax.dot_general(normed, upstream, contract, preferred_element_type=jnp.fl...  13 us
    all_to_all x1, blocking collectives, summed_on_arrival(): lax.all_to_all(parts, axis, split_axis=0, concat_axis=0, tiled=True)  9.32 us
  transfers between devices with their start and end apart: 1, of which 1 were waited for; matrix products, arithmetic and copies ran while one was open for 0% of the time, Pallas kernels for 0%

commit v1 on v0

v1 whole, which is shorter than its diff:
```python
import functools
import math

import jax
import jax.numpy as jnp
from jax import lax
from jax.experimental import pallas as pl
from jax.experimental.pallas import tpu as pltpu
from jax.sharding import Mesh
from jax.sharding import PartitionSpec as P


X, Z, CORE, DP = 4, 8, 2, 4
LANE = 128
WIRE = jnp.bfloat16
WIRE_TOP = 15.0
TAIL = 16
VMEM = pltpu.VMEM
F32 = jnp.float32


def call(kernel, out_shape, in_specs, out_specs, scalars=0, grid=(), scratch=(), flops=0, moved=0, mib=12):
    return pl.pallas_call(
        kernel,
        out_shape=out_shape,
        compiler_params=pltpu.CompilerParams(vmem_limit_bytes=mib << 20),
        grid_spec=pltpu.PrefetchScalarGridSpec(
            num_scalar_prefetch=scalars,
            grid=grid,
            in_specs=in_specs,
            out_specs=out_specs,
            scratch_shapes=list(scratch),
        ),
        cost_estimate=pl.CostEstimate(flops=flops, bytes_accessed=moved, transcendentals=0),
    )


def whole():
    return pl.BlockSpec(memory_space=VMEM)


def prep_kernel(core_ref, hidden_ref, cot_ref, send_ref, scale_ref, top_ref):
    step = pl.program_id(0)
    rows, features = hidden_ref.shape
    other = 1 - core_ref[0]
    tiles = features // LANE
    total = jnp.zeros((rows, LANE), F32)
    for i in range(tiles):
        v = hidden_ref[:, i * LANE : (i + 1) * LANE].astype(F32)
        total = total + v * v
    mean = jnp.sum(total, axis=1, keepdims=True) * (1.0 / features)
    scale = lax.rsqrt(mean + 1e-05)
    at = pl.multiple_of(step * rows, rows)
    scale_ref[pl.ds(at, rows), :] = jnp.broadcast_to(scale, (rows, LANE))
    for i in range(tiles // 2):
        src = pl.multiple_of((2 * i + other) * LANE, LANE)
        send_ref[:, i * LANE : (i + 1) * LANE] = hidden_ref[:, pl.ds(src, LANE)]
    largest = jnp.max(jnp.abs(cot_ref[...].astype(F32)), axis=0, keepdims=True)
    lanes = largest[:, :LANE]
    for i in range(1, largest.shape[1] // LANE):
        lanes = jnp.maximum(lanes, largest[:, i * LANE : (i + 1) * LANE])

    @pl.when(step == 0)
    def _():
        top_ref[...] = jnp.zeros_like(top_ref)

    top_ref[...] = jnp.maximum(top_ref[...], jnp.broadcast_to(lanes, top_ref.shape))
    last = scale_ref.shape[0] - 8
    scale_ref[last:, :] = top_ref[...]


def prep(hidden, cot, core):
    tokens, features = hidden.shape
    steps = 8
    rows = tokens // steps
    return call(
        prep_kernel,
        (
            jax.ShapeDtypeStruct((tokens, features // 2), hidden.dtype),
            jax.ShapeDtypeStruct((tokens + 8, LANE), F32),
        ),
        [
            pl.BlockSpec((rows, features), lambda i, s: (i, 0)),
            pl.BlockSpec((rows, cot.shape[1]), lambda i, s: (i, 0)),
        ],
        (
            pl.BlockSpec((rows, features // 2), lambda i, s: (i, 0)),
            pl.BlockSpec((tokens + 8, LANE), lambda i, s: (0, 0)),
        ),
        scalars=1,
        grid=(steps,),
        scratch=[VMEM((8, LANE), F32)],
        flops=2 * tokens * features,
        moved=3 * tokens * features,
        mib=56,
    )(core, hidden, cot)


def product_kernel(keep, at_ref, *refs):
    own = refs[:2]
    par_ref, so_ref, sp_ref, gain_ref, cto_ref, ctp_ref, a_ref, b_ref, normed = refs[2:]
    step = pl.program_id(0)
    tokens = par_ref.shape[0]
    half = cto_ref.shape[0] // 2
    first = at_ref[0] * (2 * Z) + at_ref[1] + 4 * step
    so = so_ref[:tokens, :]
    sp = sp_ref[:tokens, :]
    for i in range(2):
        g = gain_ref[pl.ds(first + 2 * i, 1), :]
        lanes = slice(i * LANE, (i + 1) * LANE)
        normed[:tokens, lanes] = (own[i][...].astype(F32) * so * g).astype(jnp.bfloat16)
        normed[tokens:, lanes] = (par_ref[:, lanes].astype(F32) * sp * g).astype(jnp.bfloat16)
    features = gain_ref.shape[0] * gain_ref.shape[1]
    top = jnp.maximum(jnp.max(so_ref[tokens:, :]), jnp.max(sp_ref[tokens:, :]))
    steepest = jnp.max(jnp.abs(gain_ref[...]))
    bound = jnp.maximum(2.0 * tokens * math.sqrt(features) * top * steepest, 1e-30)
    power = jnp.ceil(jnp.log(jnp.full((1, LANE), bound, F32)) * (1.0 / math.log(2.0))) - WIRE_TOP
    down = jnp.exp(power * -math.log(2.0))
    out = jnp.dot(cto_ref[...], normed[:tokens, :], preferred_element_type=F32)
    out = out + jnp.dot(ctp_ref[...], normed[tokens:, :], preferred_element_type=F32)
    for i in range(2):
        at = pl.multiple_of((2 * step + i) * half, half)
        tile = out[:, i * LANE : (i + 1) * LANE]
        if not keep:
            tile = tile * down
        a_ref[pl.ds(at, half), :] = tile[:half].astype(a_ref.dtype)
        b_ref[pl.ds(at, half), :] = tile[half:].astype(b_ref.dtype)
    tail = jnp.broadcast_to(power, (TAIL, LANE))
    a_ref[Z * half :, :] = tail.astype(a_ref.dtype)
    b_ref[Z * half :, :] = tail.astype(b_ref.dtype)


def product(hidden, par, so, sp, gain, cto, ctp, at, keep):
    tokens = par.shape[0]
    outs = cto.shape[0]
    half = outs // 2
    dtype = F32 if keep else WIRE
    shape = jax.ShapeDtypeStruct((Z * half + TAIL, LANE), dtype)
    fixed = lambda a: pl.BlockSpec(a.shape, lambda i, s: (0, 0))
    tile = lambda k: pl.BlockSpec((tokens, LANE), lambda i, s: (0, s[0] * (2 * Z) + s[1] + 4 * i + 2 * k))
    out = pl.BlockSpec(shape.shape, lambda i, s: (0, 0))
    return call(
        functools.partial(product_kernel, keep),
        (shape, shape),
        [
            tile(0),
            tile(1),
            pl.BlockSpec((tokens, 2 * LANE), lambda i, s: (0, s[0] * (Z // 2) + i)),
            fixed(so),
            fixed(sp),
            fixed(gain),
            fixed(cto),
            fixed(ctp),
        ],
        (out, out),
        scalars=1,
        grid=(Z // 2,),
        scratch=[VMEM((2 * tokens, 2 * LANE), jnp.bfloat16)],
        flops=2 * outs * 2 * tokens * Z * LANE,
        moved=4 * tokens * Z * LANE + 4 * outs * Z * LANE,
        mib=52,
    )(at, hidden, hidden, par, so, sp, gain, cto, ctp)


def up(power):
    return jnp.exp(power.astype(F32) * math.log(2.0))


def gather_kernel(own_ref, r1_ref, r2_ref, r3_ref, out_ref):
    rows = own_ref.shape[0] - TAIL
    half = rows // Z
    power = own_ref[rows : rows + 1, :]
    scales = []
    for r in (r1_ref, r2_ref, r3_ref):
        p = r[rows:, :].astype(F32)[:1, :]
        scales.append(up(p))
        power = jnp.maximum(power, p)
    power = power + 2.0
    down = jnp.exp(power * -math.log(2.0))
    tail = jnp.broadcast_to(power, (TAIL, LANE)).astype(out_ref.dtype)
    for j in range(Z):
        at = slice(j * half, (j + 1) * half)
        total = own_ref[at, :]
        for r, s in zip((r1_ref, r2_ref, r3_ref), scales):
            total = total + r[at, :].astype(F32) * s
        out_ref[j, :half, :] = (total * down).astype(out_ref.dtype)
        out_ref[j, half:, :] = tail


def gather(own, r1, r2, r3):
    half = (own.shape[0] - TAIL) // Z
    return call(
        gather_kernel,
        jax.ShapeDtypeStruct((Z, half + TAIL, LANE), WIRE),
        [whole()] * 4,
        whole(),
        flops=8 * own.size,
        moved=12 * own.size,
    )(own, r1, r2, r3)


def finish_kernel(at_ref, weight_ref, a_ref, b_ref, *refs):
    outs, squares_ref, tile = refs[:DP], refs[DP], refs[DP + 1]
    half = a_ref.shape[1] - TAIL
    weight = weight_ref[0]
    squares = jnp.zeros((1, LANE), F32)
    for n, r in enumerate((a_ref, b_ref)):
        scales = [up(r[j, half:, :].astype(F32)[:1, :]) * weight for j in range(Z)]
        total = r[0, :half, :].astype(F32) * scales[0]
        for j in range(1, Z):
            total = total + r[j, :half, :].astype(F32) * scales[j]
        tile[n * half : (n + 1) * half, :] = total
        squares = squares + jnp.sum(total * total, axis=0, keepdims=True)
    rows = 2 * half // DP
    for k in range(DP):
        owner = jnp.bitwise_and(at_ref[0] + k, DP - 1)
        outs[k][...] = tile[pl.ds(pl.multiple_of(owner * rows, rows), rows), :]
    squares_ref[...] = jnp.broadcast_to(squares[None], squares_ref.shape)


def finish(a, b, dp, weight):
    half = a.shape[1] - TAIL
    rows = 2 * half // DP
    block = jax.ShapeDtypeStruct((rows, LANE), F32)
    return call(
        finish_kernel,
        (block,) * DP + (jax.ShapeDtypeStruct((Z * CORE, 1, LANE), F32),),
        [pl.BlockSpec(memory_space=pltpu.SMEM), whole(), whole()],
        (whole(),) * (DP + 1),
        scalars=1,
        scratch=[VMEM((2 * half, LANE), F32)],
        flops=4 * a.size,
        moved=4 * a.size,
    )(dp, weight, a, b)


def pass_kernel(in_ref, out_ref):
    out_ref[...] = jnp.broadcast_to(jnp.sum(in_ref[...], axis=0, keepdims=True), out_ref.shape)


def combine_kernel(clip_bound, at_ref, squares_ref, *refs):
    blocks, out_ref = refs[:DP], refs[DP]
    total = None
    for k in range(DP):
        example = jnp.bitwise_and(at_ref[0] + DP - k, DP - 1)
        squares = jnp.sum(squares_ref[pl.ds(example * X, X)])
        factor = jnp.minimum(1.0, clip_bound * lax.rsqrt(jnp.full((1, LANE), squares, F32) + 1e-06))
        term = blocks[k][...] * factor
        total = term if total is None else total + term
    out_ref[...] = total.T


def turn(n, k):
    return [(i, (i + k) % n) for i in range(n)]


def per_device(hidden, norm_gain, cotangent, loss_weight):
    hidden, cot = hidden[0], cotangent[0]
    tokens, features = hidden.shape
    outs = cot.shape[1]
    doc_length = tokens * X * Z * CORE
    x, core, dp = (lax.axis_index(n).astype(jnp.int32) for n in ("x", "core", "dp"))
    swap = functools.partial(lax.ppermute, axis_name="core", perm=turn(CORE, 1))
    send, so = prep(hidden, cot, core[None])
    par = swap(send)
    cto = cot.T
    ctp = swap(cto)
    sp = swap(so)
    gain = norm_gain.reshape(features // LANE, LANE)
    weight = loss_weight * (1.0 / math.sqrt(doc_length))

    def block(k):
        at = jnp.stack([jnp.bitwise_and(x + k, X - 1), core])
        return product(hidden, par, so, sp, gain, cto, ctp, at, k == 0)

    blocks = {k: block(k) for k in (1, 3, 2, 0)}
    summed = []
    for chunk in range(2):
        arrived = [lax.ppermute(blocks[k][chunk], "x", turn(X, k)) for k in (1, 3, 2)]
        ready = gather(blocks[0][chunk], *arrived)
        summed.append(lax.all_to_all(ready, "z", split_axis=0, concat_axis=0, tiled=True))
    *tiles, squares = finish(*summed, dp[None], weight)
    arrived = [tiles[0]] + [lax.ppermute(tiles[k], "dp", turn(DP, k)) for k in range(1, DP)]
    squares = lax.all_to_all(squares, ("z", "core"), split_axis=0, concat_axis=0, tiled=True)
    squares = call(pass_kernel, jax.ShapeDtypeStruct((DP * X, 1, LANE), F32), [whole()], whole())(squares)
    squares = lax.all_to_all(squares, ("dp", "x"), split_axis=0, concat_axis=0, tiled=True)
    clip_bound = math.sqrt(features * outs)
    return call(
        functools.partial(combine_kernel, clip_bound),
        jax.ShapeDtypeStruct((LANE, outs // DP), F32),
        [whole()] * (DP + 1),
        whole(),
        scalars=1,
    )(dp[None], squares, *arrived)


def solution(mesh):
    fine = Mesh(mesh.devices.reshape(DP, X, Z, CORE), ("dp", "x", "z", "core"))
    ctx = ("x", "z", "core")
    in_specs = (P("dp", ctx, None), P(), P("dp", ctx, None), P("dp"))
    out_specs = P(ctx, "dp")
    return jax.shard_map(
        per_device, mesh=fine, in_specs=in_specs, out_specs=out_specs, check_vma=False
    )
```

time: 258 us -> 145 us (0.56)
  waiting for transfers between devices: 190 us -> 57.5 us
  Pallas kernels: 0 us -> 34.4 us
  starting transfers between devices: 0.01 us -> 27.8 us
  between operations: 14.8 us -> 0.7 us
  matrix products: 13 us -> 0 us
  blocking collectives: 30.3 us -> 21.2 us
  other arithmetic: 9.02 us -> 0.15 us
    reduce_scatter x1 -> x0, waiting for transfers between devices: 190 us -> none  [per_device(): lax.psum_scatter(weight * lax.dot_general(normed, upstream, contract, pre...]
    ppermute x0 -> x12, waiting for transfers between devices: none -> 39.5 us  [the longest x6 32.3 us: per_device(): lax.ppermute(blocks[k][chunk], 'x', turn(X, k))]
    pallas_call x0 -> x10, Pallas kernels: none -> 34.4 us  [the longest x4 21.8 us: product(): call(functools.partial(product_kernel, keep), (shape, shape), [tile(0), t...]
    all_to_all x0 -> x2, waiting for transfers between devices: none -> 18 us  [per_device(): lax.all_to_all(ready, 'z', split_axis=0, concat_axis=0, tiled=True)]
    all_to_all x0 -> x2, starting transfers between devices: none -> 14.7 us  [per_device(): lax.all_to_all(ready, 'z', split_axis=0, concat_axis=0, tiled=True)]
    ppermute x0 -> x12, starting transfers between devices: none -> 13 us  [the longest x6 4.78 us: per_device(): lax.ppermute(blocks[k][chunk], 'x', turn(X, k))]
    dot_general x1 -> x0, matrix products: 13 us -> none  [per_device(): lax.dot_general(normed, upstream, contract, preferred_element_type=jnp.fl...]
    all_to_all x2, blocking collectives: 30.3 us -> 21.2 us  [the longest x1 10.8 us: per_device(): lax.all_to_all(squares, ('z', 'core'), split_axis=0, concat_axis=0, tiled...]
  transfers between devices with their start and end apart: 1 -> 14, of which waited for: 1 -> 7; matrix products, arithmetic and copies ran while one was open for 0% -> 0% of each run, Pallas kernels for 0% -> 12%
where the time goes in v1:
time: 145 us; the launch traced here: 144 us
  waiting for transfers between devices  57.5 us (40%)
  Pallas kernels  34.4 us (24%)
  starting transfers between devices  27.8 us (19%)
  blocking collectives  21.2 us (15%)
  local copies, waits for them, and re-layouts  2.41 us (2%)
    ppermute x6, waiting for transfers between devices, per_device(): lax.ppermute(blocks[k][chunk], 'x', turn(X, k))  32.3 us
    pallas_call x4, Pallas kernels, product(): call(functools.partial(product_kernel, keep), (shape, shape), [tile(0), t...  21.8 us
    all_to_all x2, waiting for transfers between devices, per_device(): lax.all_to_all(ready, 'z', split_axis=0, concat_axis=0, tiled=True)  18 us
    all_to_all x2, starting transfers between devices, per_device(): lax.all_to_all(ready, 'z', split_axis=0, concat_axis=0, tiled=True)  14.7 us
    all_to_all x1, blocking collectives, per_device(): lax.all_to_all(squares, ('z', 'core'), split_axis=0, concat_axis=0, tiled...  10.8 us
    all_to_all x1, blocking collectives, per_device(): lax.all_to_all(squares, ('dp', 'x'), split_axis=0, concat_axis=0, tiled=T...  10.4 us
    pallas_call x1, Pallas kernels, prep(): call(prep_kernel, (jax.ShapeDtypeStruct((tokens, features // 2), hidden.d...  9.03 us
    ppermute x1, waiting for transfers between devices, per_device(): sp = swap(so)  7.16 us
  transfers between devices with their start and end apart: 14, of which 7 were waited for; matrix products, arithmetic and copies ran while one was open for 0% of the time, Pallas kernels for 12%

profile of v1, /device:TPU:1, one launch (start us, length us, event | category | flops | bytes accessed | tf_op | source)
XLA Modules:
  0.0 144.1 jit_solution(17686796681376999425)
XLA Ops:
  0.0 0.0 copy-start.4
  0.0 0.0 copy-start.3
  0.0 9.0 %shard_map.46 = (bf16[512,4096]{1,0:T(8,128)(2,1)}, f32[520,128]{1,0:T(8,128)}) custom-call(s32[1]{0:T(128)} %bitcast.2.core_ref, bf16[512,8192]{1,0:T(8,128)(2,1)} %bitcast.21, bf16[512,512]{1,0:T(8,128)(2,1)} %bitcast.30), custom_call_target="tpu_custom_call" | custom-call | flops 8388608 | bytes 12582912 | tf_op jit(solution)/shard_map/pallas_call | solution.py:76
  9.0 3.2 %collective-permute-start = (bf16[512,4096]{1,0:T(8,128)(2,1)}, bf16[512,4096]{1,0:T(8,128)(2,1)}, u32[]{:S(2)}, u32[]{:S(2)}) collective-permute-start(bf16[512,4096]{1,0:T(8,128)(2,1)} %get-tuple-element.20), channel_id=1, source_target_pairs={{0,1},{1,0},{2,3},{3,2},{4,5},{5,4},{6,7},{7,6},{8,9},{9,8},{10,11... | collective-permute-start | bytes 12582920 | tf_op jit(solution)/shard_map/ppermute | solution.py:265
  12.2 0.0 copy-done.4
  12.2 0.2 copy.5
  12.5 0.1 collective-permute-start.2
  12.6 0.5 collective-permute-start.1
  13.1 0.1 pad_add_fusion.2
  13.1 0.1 pad_add_fusion
  13.2 7.2 %collective-permute-done.1.refs_4_ = f32[520,128]{1,0:T(8,128)S(1)} collective-permute-done((f32[520,128]{1,0:T(8,128)}, f32[520,128]{1,0:T(8,128)S(1)}, u32[]{:S(2)}, u32[]{:S(2)}) %collective-permute-start.1) | collective-permute-done | bytes 266272 | tf_op jit(solution)/shard_map/ppermute | solution.py:268
  20.4 0.0 collective-permute-done.2.refs_7_
  20.4 0.0 collective-permute-done.refs_2_
  20.4 0.0 copy-done.3
  20.4 0.0 copy-start
  20.4 0.9 copy-done
  21.3 5.4 %shard_map.50 = (bf16[2064,128]{1,0:T(8,128)(2,1)}, bf16[2064,128]{1,0:T(8,128)(2,1)}) custom-call(s32[2]{0:T(128)S(1)} %get-tuple-element.38.at_ref, bf16[512,8192]{1,0:T(8,128)(2,1)} %bitcast.22, bf16[512,8192]{1,0:T(8,128)(2,1)} %bitcast.23, bf16[512,4096]{1,0:T(8,128)(2,1)} %collective-permute-done.refs_2_, f32[520,128]{1,0:T(8,128)S(1)} %copy-done, ...), custom_call_target="tpu_custom_call" | custom-call | flops 1073741824 | bytes 4194304 | tf_op jit(solution)/shard_map/pallas_call | solution.py:142
  26.7 1.0 collective-permute-start.8
  27.7 5.4 %shard_map.49 = (bf16[2064,128]{1,0:T(8,128)(2,1)}, bf16[2064,128]{1,0:T(8,128)(2,1)}) custom-call(s32[2]{0:T(128)S(1)} %get-tuple-element.37.at_ref, bf16[512,8192]{1,0:T(8,128)(2,1)} %bitcast.24, bf16[512,8192]{1,0:T(8,128)(2,1)} %bitcast.25, bf16[512,4096]{1,0:T(8,128)(2,1)} %collective-permute-done.refs_2_, f32[520,128]{1,0:T(8,128)S(1)} %copy-done, ...), custom_call_target="tpu_custom_call" | custom-call | flops 1073741824 | bytes 4194304 | tf_op jit(solution)/shard_map/pallas_call | solution.py:142
  33.1 0.9 collective-permute-start.7
  33.9 5.4 %shard_map.48 = (bf16[2064,128]{1,0:T(8,128)(2,1)}, bf16[2064,128]{1,0:T(8,128)(2,1)}) custom-call(s32[2]{0:T(128)S(1)} %get-tuple-element.36.at_ref, bf16[512,8192]{1,0:T(8,128)(2,1)} %bitcast.26, bf16[512,8192]{1,0:T(8,128)(2,1)} %bitcast.27, bf16[512,4096]{1,0:T(8,128)(2,1)} %collective-permute-done.refs_2_, f32[520,128]{1,0:T(8,128)S(1)} %copy-done, ...), custom_call_target="tpu_custom_call" | custom-call | flops 1073741824 | bytes 4194304 | tf_op jit(solution)/shard_map/pallas_call | solution.py:142
  39.3 0.6 collective-permute-start.6
  39.9 0.0 copy-start.5
  39.9 0.0 copy-start.6
  39.9 0.0 copy-start.7
  39.9 5.7 %shard_map.47 = (f32[2064,128]{1,0:T(8,128)}, f32[2064,128]{1,0:T(8,128)}) custom-call(s32[2]{0:T(128)S(1)} %get-tuple-element.35.at_ref, bf16[512,8192]{1,0:T(8,128)(2,1)} %bitcast.28, bf16[512,8192]{1,0:T(8,128)(2,1)} %bitcast.29, bf16[512,4096]{1,0:T(8,128)(2,1)} %collective-permute-done.refs_2_, f32[520,128]{1,0:T(8,128)S(1)} %copy-done, ...), custom_call_target="tpu_custom_call" | custom-call | flops 1073741824 | bytes 4194304 | tf_op jit(solution)/shard_map/pallas_call | solution.py:142
  45.6 0.0 copy-start.1
  45.6 0.0 collective-permute-done.8.r3_ref
  45.6 5.7 %collective-permute-done.7.r2_ref = bf16[2064,128]{1,0:T(8,128)(2,1)S(1)} collective-permute-done((bf16[2064,128]{1,0:T(8,128)(2,1)}, bf16[2064,128]{1,0:T(8,128)(2,1)S(1)}, u32[]{:S(2)}, u32[]{:S(2)}) %collective-permute-start.7) | collective-permute-done | bytes 528416 | tf_op jit(solution)/shard_map/ppermute | solution.py:279
  51.4 2.0 %collective-permute-done.6.r1_ref = bf16[2064,128]{1,0:T(8,128)(2,1)S(1)} collective-permute-done((bf16[2064,128]{1,0:T(8,128)(2,1)}, bf16[2064,128]{1,0:T(8,128)(2,1)S(1)}, u32[]{:S(2)}, u32[]{:S(2)}) %collective-permute-start.6) | collective-permute-done | bytes 528416 | tf_op jit(solution)/shard_map/ppermute | solution.py:279
  53.4 0.0 copy-start.2
  53.4 1.2 copy-done.2
  54.6 1.2 shard_map.52
  55.8 8.2 %all-to-all-start.1 = ((bf16[8,272,128]{2,1,0:T(8,128)(2,1)}), bf16[8,272,128]{2,1,0:T(8,128)(2,1)S(1)}, u32[]{:S(2)}, u32[]{:S(2)}) async-start(bf16[8,272,128]{2,1,0:T(8,128)(2,1)} %shard_map.52), calls=%async_computation.1 | async-start | bytes 1114112 | tf_op jit(solution)/shard_map/all_to_all | solution.py:281
  64.0 0.0 copy-done.5
  64.0 0.1 collective-permute-start.5
  64.1 0.0 copy-done.6
  64.1 2.2 %collective-permute-start.4 = (bf16[2064,128]{1,0:T(8,128)(2,1)S(1)}, bf16[2064,128]{1,0:T(8,128)(2,1)S(1)}, u32[]{:S(2)}, u32[]{:S(2)}) collective-permute-start(bf16[2064,128]{1,0:T(8,128)(2,1)S(1)} %copy-done.6), channel_id=1, source_target_pairs={{0,48},{16,0},{32,16},{48,32},{1,49},{17,1},{33,17},{49,33},{2,50}... | collective-permute-start | bytes 1585160 | tf_op jit(solution)/shard_map/ppermute | solution.py:279
  66.3 0.0 copy-done.7
  66.3 0.0 collective-permute-start.3
  66.3 10.8 %collective-permute-done.5.r3_ref = bf16[2064,128]{1,0:T(8,128)(2,1)S(1)} collective-permute-done((bf16[2064,128]{1,0:T(8,128)(2,1)S(1)}, bf16[2064,128]{1,0:T(8,128)(2,1)S(1)}, u32[]{:S(2)}, u32[]{:S(2)}) %collective-permute-start.5) | collective-permute-done | bytes 528416 | tf_op jit(solution)/shard_map/ppermute | solution.py:279
  77.1 11.4 %collective-permute-done.4.r2_ref = bf16[2064,128]{1,0:T(8,128)(2,1)S(1)} collective-permute-done((bf16[2064,128]{1,0:T(8,128)(2,1)S(1)}, bf16[2064,128]{1,0:T(8,128)(2,1)S(1)}, u32[]{:S(2)}, u32[]{:S(2)}) %collective-permute-start.4) | collective-permute-done | bytes 528416 | tf_op jit(solution)/shard_map/ppermute | solution.py:279
  88.5 2.3 %collective-permute-done.3.r1_ref = bf16[2064,128]{1,0:T(8,128)(2,1)S(1)} collective-permute-done((bf16[2064,128]{1,0:T(8,128)(2,1)S(1)}, bf16[2064,128]{1,0:T(8,128)(2,1)S(1)}, u32[]{:S(2)}, u32[]{:S(2)}) %collective-permute-start.3) | collective-permute-done | bytes 528416 | tf_op jit(solution)/shard_map/ppermute | solution.py:279
  90.8 0.0 copy-done.1
  90.8 1.2 shard_map.51
  92.0 0.0 all-to-all-done.1.b_ref
  92.0 6.6 %all-to-all-start = ((bf16[8,272,128]{2,1,0:T(8,128)(2,1)}), bf16[8,272,128]{2,1,0:T(8,128)(2,1)S(1)}, u32[]{:S(2)}, u32[]{:S(2)}) async-start(bf16[8,272,128]{2,1,0:T(8,128)(2,1)} %shard_map.51), calls=%async_computation | async-start | bytes 1114112 | tf_op jit(solution)/shard_map/all_to_all | solution.py:281
  99.2 18.0 %all-to-all-done.a_ref = bf16[8,272,128]{2,1,0:T(8,128)(2,1)S(1)} async-done(((bf16[8,272,128]{2,1,0:T(8,128)(2,1)}), bf16[8,272,128]{2,1,0:T(8,128)(2,1)S(1)}, u32[]{:S(2)}, u32[]{:S(2)}) %all-to-all-start) | async-done | bytes 557088 | tf_op jit(solution)/shard_map/all_to_all | solution.py:281
  117.2 0.3 shard_map.53
  117.5 3.0 %collective-permute-start.10 = (f32[128,128]{1,0:T(8,128)S(1)}, f32[128,128]{1,0:T(8,128)S(1)}, u32[]{:S(2)}, u32[]{:S(2)}) collective-permute-start(f32[128,128]{1,0:T(8,128)S(1)} %get-tuple-element.33), channel_id=1, source_target_pairs={{0,128},{64,192},{128,0},{192,64},{1,129},{65,193},{129,1},{193,65... | collective-permute-start | bytes 196616 | tf_op jit(solution)/shard_map/ppermute | solution.py:283
  120.5 0.8 collective-permute-start.11
  121.3 0.7 collective-permute-start.9
  122.0 10.8 %all_to_all.20.in_ref = f32[16,1,128]{2,1,0:T(1,128)S(1)} all-to-all(f32[16,1,128]{2,1,0:T(1,128)S(1)} %get-tuple-element.30), channel_id=1, replica_groups=mesh['dp'=4,'x'=4,'z'=8,'core'=2] {'z','core'}, dimensions={0} | all-to-all | bytes 16384 | tf_op jit(solution)/shard_map/all_to_all | solution.py:284
  132.8 10.4 %all_to_all.21.squares_ref = f32[16,1,128]{2,1,0:T(1,128)S(1)} all-to-all(f32[16,1,128]{2,1,0:T(1,128)S(1)} %shard_map.54), channel_id=1, replica_groups=mesh['dp'=4,'x'=4,'z'=8,'core'=2] {'dp','x'}, dimensions={0} | all-to-all | bytes 16384 | tf_op jit(solution)/shard_map/all_to_all | solution.py:286
  143.2 0.0 collective-permute-done.10.refs_2_
  143.2 0.0 collective-permute-done.11.refs_3_
  143.2 0.0 collective-permute-done.9.refs_1_
  143.2 0.9 shard_map.55
  (1 shorter events, 0.0 us)
Async XLA Ops:
  0.0 12.2 %copy-start.4 = (bf16[1,512,512]{2,1,0:T(8,128)(2,1)S(1)}, bf16[1,512,512]{2,1,0:T(8,128)(2,1)}, u32[]{:S(2)}) copy-start(bf16[1,512,512]{2,1,0:T(8,128)(2,1)} %param.6) | copy-start | bytes 1572868
  0.0 20.4 %copy-start.3 = (f32[8192]{0:T(1024)S(1)}, f32[8192]{0:T(1024)}, u32[]{:S(2)}) copy-start(f32[8192]{0:T(1024)} %param.5) | copy-start | bytes 98308
  9.0 11.3 %collective-permute-start = (bf16[512,4096]{1,0:T(8,128)(2,1)}, bf16[512,4096]{1,0:T(8,128)(2,1)}, u32[]{:S(2)}, u32[]{:S(2)}) collective-permute-start(bf16[512,4096]{1,0:T(8,128)(2,1)} %get-tuple-element.20), channel_id=1, source_target_pairs={{0,1},{1,0},{2,3},{3,2},{4,5},{5,4},{6,7},{7,6},{8,9},{9,8},{10,11... | collective-permute-start | bytes 12582920 | tf_op jit(solution)/shard_map/ppermute | solution.py:265
  12.5 7.9 %collective-permute-start.2 = (bf16[512,512]{1,0:T(8,128)(2,1)S(1)}, bf16[512,512]{1,0:T(8,128)(2,1)S(1)}, u32[]{:S(2)}, u32[]{:S(2)}) collective-permute-start(bf16[512,512]{1,0:T(8,128)(2,1)S(1)} %bitcast.12), channel_id=1, source_target_pairs={{0,1},{1,0},{2,3},{3,2},{4,5},{5,4},{6,7},{7,6},{8,9},{9,8},{10,11... | collective-permute-start | bytes 1572872 | tf_op jit(solution)/shard_map/ppermute | solution.py:267
  12.6 7.8 %collective-permute-start.1 = (f32[520,128]{1,0:T(8,128)}, f32[520,128]{1,0:T(8,128)S(1)}, u32[]{:S(2)}, u32[]{:S(2)}) collective-permute-start(f32[520,128]{1,0:T(8,128)} %get-tuple-element.21.refs_3_), channel_id=1, source_target_pairs={{0,1},{1,0},{2,3},{3,2},{4,5},{5,4},{6,7},{7,6},{8,9},{9,8},{10,11... | collective-permute-start | bytes 798728 | tf_op jit(solution)/shard_map/ppermute | solution.py:268
  20.4 1.0 copy-start
  26.7 18.9 %collective-permute-start.8 = (bf16[2064,128]{1,0:T(8,128)(2,1)}, bf16[2064,128]{1,0:T(8,128)(2,1)S(1)}, u32[]{:S(2)}, u32[]{:S(2)}) collective-permute-start(bf16[2064,128]{1,0:T(8,128)(2,1)} %get-tuple-element.29), channel_id=1, source_target_pairs={{0,32},{16,48},{32,0},{48,16},{1,33},{17,49},{33,1},{49,17},{2,34}... | collective-permute-start | bytes 1585160 | tf_op jit(solution)/shard_map/ppermute | solution.py:279
  33.1 18.3 %collective-permute-start.7 = (bf16[2064,128]{1,0:T(8,128)(2,1)}, bf16[2064,128]{1,0:T(8,128)(2,1)S(1)}, u32[]{:S(2)}, u32[]{:S(2)}) collective-permute-start(bf16[2064,128]{1,0:T(8,128)(2,1)} %get-tuple-element.28), channel_id=1, source_target_pairs={{0,48},{16,0},{32,16},{48,32},{1,49},{17,1},{33,17},{49,33},{2,50}... | collective-permute-start | bytes 1585160 | tf_op jit(solution)/shard_map/ppermute | solution.py:279
  39.3 14.1 %collective-permute-start.6 = (bf16[2064,128]{1,0:T(8,128)(2,1)}, bf16[2064,128]{1,0:T(8,128)(2,1)S(1)}, u32[]{:S(2)}, u32[]{:S(2)}) collective-permute-start(bf16[2064,128]{1,0:T(8,128)(2,1)} %get-tuple-element.27), channel_id=1, source_target_pairs={{0,16},{16,32},{32,48},{48,0},{1,17},{17,33},{33,49},{49,1},{2,18}... | collective-permute-start | bytes 1585160 | tf_op jit(solution)/shard_map/ppermute | solution.py:279
  39.9 24.0 %copy-start.5 = (bf16[2064,128]{1,0:T(8,128)(2,1)S(1)}, bf16[2064,128]{1,0:T(8,128)(2,1)}, u32[]{:S(2)}) copy-start(bf16[2064,128]{1,0:T(8,128)(2,1)} %get-tuple-element.25) | copy-start | bytes 1585156
  39.9 24.2 %copy-start.6 = (bf16[2064,128]{1,0:T(8,128)(2,1)S(1)}, bf16[2064,128]{1,0:T(8,128)(2,1)}, u32[]{:S(2)}) copy-start(bf16[2064,128]{1,0:T(8,128)(2,1)} %get-tuple-element.24) | copy-start | bytes 1585156
  39.9 26.3 %copy-start.7 = (bf16[2064,128]{1,0:T(8,128)(2,1)S(1)}, bf16[2064,128]{1,0:T(8,128)(2,1)}, u32[]{:S(2)}) copy-start(bf16[2064,128]{1,0:T(8,128)(2,1)} %get-tuple-element.23) | copy-start | bytes 1585156
  45.6 45.2 %copy-start.1 = (f32[2064,128]{1,0:T(8,128)S(1)}, f32[2064,128]{1,0:T(8,128)}, u32[]{:S(2)}) copy-start(f32[2064,128]{1,0:T(8,128)} %get-tuple-element.22.own_ref) | copy-start | bytes 3170308
  53.4 1.2 copy-start.2
  55.8 36.2 %all-to-all-start.1 = ((bf16[8,272,128]{2,1,0:T(8,128)(2,1)}), bf16[8,272,128]{2,1,0:T(8,128)(2,1)S(1)}, u32[]{:S(2)}, u32[]{:S(2)}) async-start(bf16[8,272,128]{2,1,0:T(8,128)(2,1)} %shard_map.52), calls=%async_computation.1 | async-start | bytes 1114112 | tf_op jit(solution)/shard_map/all_to_all | solution.py:281
  64.0 13.1 %collective-permute-start.5 = (bf16[2064,128]{1,0:T(8,128)(2,1)S(1)}, bf16[2064,128]{1,0:T(8,128)(2,1)S(1)}, u32[]{:S(2)}, u32[]{:S(2)}) collective-permute-start(bf16[2064,128]{1,0:T(8,128)(2,1)S(1)} %copy-done.5), channel_id=1, source_target_pairs={{0,32},{16,48},{32,0},{48,16},{1,33},{17,49},{33,1},{49,17},{2,34}... | collective-permute-start | bytes 1585160 | tf_op jit(solution)/shard_map/ppermute | solution.py:279
  64.1 24.4 %collective-permute-start.4 = (bf16[2064,128]{1,0:T(8,128)(2,1)S(1)}, bf16[2064,128]{1,0:T(8,128)(2,1)S(1)}, u32[]{:S(2)}, u32[]{:S(2)}) collective-permute-start(bf16[2064,128]{1,0:T(8,128)(2,1)S(1)} %copy-done.6), channel_id=1, source_target_pairs={{0,48},{16,0},{32,16},{48,32},{1,49},{17,1},{33,17},{49,33},{2,50}... | collective-permute-start | bytes 1585160 | tf_op jit(solution)/shard_map/ppermute | solution.py:279
  66.3 24.6 %collective-permute-start.3 = (bf16[2064,128]{1,0:T(8,128)(2,1)S(1)}, bf16[2064,128]{1,0:T(8,128)(2,1)S(1)}, u32[]{:S(2)}, u32[]{:S(2)}) collective-permute-start(bf16[2064,128]{1,0:T(8,128)(2,1)S(1)} %copy-done.7), channel_id=1, source_target_pairs={{0,16},{16,32},{32,48},{48,0},{1,17},{17,33},{33,49},{49,1},{2,18}... | collective-permute-start | bytes 1585160 | tf_op jit(solution)/shard_map/ppermute | solution.py:279
  92.0 25.2 %all-to-all-start = ((bf16[8,272,128]{2,1,0:T(8,128)(2,1)}), bf16[8,272,128]{2,1,0:T(8,128)(2,1)S(1)}, u32[]{:S(2)}, u32[]{:S(2)}) async-start(bf16[8,272,128]{2,1,0:T(8,128)(2,1)} %shard_map.51), calls=%async_computation | async-start | bytes 1114112 | tf_op jit(solution)/shard_map/all_to_all | solution.py:281
  117.5 25.7 %collective-permute-start.10 = (f32[128,128]{1,0:T(8,128)S(1)}, f32[128,128]{1,0:T(8,128)S(1)}, u32[]{:S(2)}, u32[]{:S(2)}) collective-permute-start(f32[128,128]{1,0:T(8,128)S(1)} %get-tuple-element.33), channel_id=1, source_target_pairs={{0,128},{64,192},{128,0},{192,64},{1,129},{65,193},{129,1},{193,65... | collective-permute-start | bytes 196616 | tf_op jit(solution)/shard_map/ppermute | solution.py:283
  120.5 22.7 %collective-permute-start.11 = (f32[128,128]{1,0:T(8,128)S(1)}, f32[128,128]{1,0:T(8,128)S(1)}, u32[]{:S(2)}, u32[]{:S(2)}) collective-permute-start(f32[128,128]{1,0:T(8,128)S(1)} %get-tuple-element.34), channel_id=1, source_target_pairs={{0,192},{64,0},{128,64},{192,128},{1,193},{65,1},{129,65},{193,129... | collective-permute-start | bytes 196616 | tf_op jit(solution)/shard_map/ppermute | solution.py:283
  121.3 21.9 %collective-permute-start.9 = (f32[128,128]{1,0:T(8,128)S(1)}, f32[128,128]{1,0:T(8,128)S(1)}, u32[]{:S(2)}, u32[]{:S(2)}) collective-permute-start(f32[128,128]{1,0:T(8,128)S(1)} %get-tuple-element.32), channel_id=1, source_target_pairs={{0,64},{64,128},{128,192},{192,0},{1,65},{65,129},{129,193},{193,1... | collective-permute-start | bytes 196616 | tf_op jit(solution)/shard_map/ppermute | solution.py:283

commit v2 on v0

v2 whole, which is shorter than its diff:
```python
import functools
import math

import jax
import jax.numpy as jnp
from jax import lax
from jax.experimental import pallas as pl
from jax.experimental.pallas import tpu as pltpu
from jax.sharding import Mesh
from jax.sharding import PartitionSpec as P


X, Z, CORE, DP = 4, 8, 2, 4
LANE = 128
WIRE = jnp.bfloat16
VMEM = pltpu.VMEM
F32 = jnp.float32
HALVES = 2
PIECES = 4


def call(kernel, out_shape, in_specs, out_specs, scalars=0, scratch=(), flops=0, moved=0, mib=12):
    return pl.pallas_call(
        kernel,
        out_shape=out_shape,
        compiler_params=pltpu.CompilerParams(vmem_limit_bytes=mib << 20),
        grid_spec=pltpu.PrefetchScalarGridSpec(
            num_scalar_prefetch=scalars,
            grid=(),
            in_specs=in_specs,
            out_specs=out_specs,
            scratch_shapes=list(scratch),
        ),
        cost_estimate=pl.CostEstimate(flops=flops, bytes_accessed=moved, transcendentals=0),
    )


def whole():
    return pl.BlockSpec(memory_space=VMEM)


def prep_kernel(half, at_ref, hidden_ref, gain_ref, own_ref, send_ref):
    rows = own_ref.shape[0] // PIECES
    features = hidden_ref.shape[1]
    tiles = features // LANE
    core = at_ref[2]
    for n in range(PIECES):
        at = slice((half * PIECES + n) * rows, (half * PIECES + n + 1) * rows)
        total = jnp.zeros((rows, LANE), F32)
        for i in range(tiles):
            v = hidden_ref[at, i * LANE : (i + 1) * LANE].astype(F32)
            total = total + v * v
        mean = jnp.sum(total, axis=1, keepdims=True) * (1.0 / features)
        scale = jnp.broadcast_to(lax.rsqrt(mean + 1e-05), (rows, LANE))
        for out, parity in ((send_ref, 1 - core), (own_ref, core)):
            for i in range(tiles // 2):
                tile = 2 * i + parity
                v = hidden_ref[at, pl.ds(pl.multiple_of(tile * LANE, LANE), LANE)].astype(F32)
                v = v * scale * gain_ref[pl.ds(tile, 1), :]
                out[n * rows : (n + 1) * rows, i * LANE : (i + 1) * LANE] = v.astype(out.dtype)


def prep(half, hidden, gain, at):
    tokens, features = hidden.shape
    rows = tokens // HALVES
    part = jax.ShapeDtypeStruct((rows, features // 2), jnp.bfloat16)
    return call(
        functools.partial(prep_kernel, half),
        (part, part),
        [whole(), whole()],
        (whole(), whole()),
        scalars=1,
        flops=4 * rows * features,
        moved=4 * rows * features,
        mib=14,
    )(at, hidden, gain)


def product_kernel(turns, at_ref, *refs):
    owner = jnp.bitwise_and(at_ref[0] + turns, X - 1)
    tokens = refs[: 2 * HALVES]
    cot_refs = refs[2 * HALVES : 2 * HALVES + 2]
    outs = refs[2 * HALVES + 2 :]
    half = cot_refs[0].shape[0] // 2
    rows = tokens[0].shape[0]
    for p in range(Z // 2):
        lanes = pl.ds(pl.multiple_of(owner * (Z * LANE) + p * 2 * LANE, 2 * LANE), 2 * LANE)
        total = None
        for n, t in enumerate(tokens):
            c = cot_refs[n // HALVES][:, (n % HALVES) * rows : (n % HALVES + 1) * rows]
            term = jnp.dot(c, t[:, lanes], preferred_element_type=F32)
            total = term if total is None else total + term
        for i in range(2):
            at = slice((2 * p + i) * half, (2 * p + i + 1) * half)
            tile = total[:, i * LANE : (i + 1) * LANE]
            outs[0][at, :] = tile[:half].astype(outs[0].dtype)
            outs[1][at, :] = tile[half:].astype(outs[1].dtype)


def product(turns, own, par, cto, ctp, at):
    outs = cto.shape[0]
    tokens = 2 * cto.shape[1]
    shape = jax.ShapeDtypeStruct((Z * outs // 2, LANE), WIRE if turns else F32)
    return call(
        functools.partial(product_kernel, turns),
        (shape, shape),
        [whole()] * (2 * HALVES + 2),
        (whole(), whole()),
        scalars=1,
        flops=2 * outs * tokens * Z * LANE,
        moved=4 * tokens * Z * LANE,
        mib=14,
    )(at, *own, *par, cto, ctp)


def gather_kernel(at_ref, own_ref, r1_ref, r2_ref, r3_ref, out_ref, mine_ref):
    half = own_ref.shape[0] // Z

    def total(at):
        value = own_ref[at, :]
        for r in (r1_ref, r2_ref, r3_ref):
            value = value + r[at, :].astype(F32)
        return value

    for j in range(Z):
        out_ref[j] = total(slice(j * half, (j + 1) * half)).astype(out_ref.dtype)
    mine_ref[...] = total(pl.ds(pl.multiple_of(at_ref[1] * half, half), half))


def gather(own, r1, r2, r3, at):
    half = own.shape[0] // Z
    return call(
        gather_kernel,
        (jax.ShapeDtypeStruct((Z, half, LANE), WIRE), jax.ShapeDtypeStruct((half, LANE), F32)),
        [whole()] * 4,
        (whole(), whole()),
        scalars=1,
        flops=4 * own.size,
        moved=12 * own.size,
    )(at, own, r1, r2, r3)


def finish_kernel(at_ref, weight_ref, *refs):
    mine, arrived, outs = refs[:2], refs[2:4], refs[4 : 4 + DP]
    squares_ref, tile = refs[4 + DP :]
    half = mine[0].shape[0]
    weight = weight_ref[0]
    squares = jnp.zeros((1, LANE), F32)
    for n in range(2):
        total = mine[n][...]
        for j in range(Z):
            other = jnp.where(at_ref[1] == j, 0.0, 1.0)
            total = total + arrived[n][j].astype(F32) * other
        total = total * weight
        tile[n * half : (n + 1) * half, :] = total
        squares = squares + jnp.sum(total * total, axis=0, keepdims=True)
    rows = 2 * half // DP
    for k in range(DP):
        owner = jnp.bitwise_and(at_ref[3] + k, DP - 1)
        outs[k][...] = tile[pl.ds(pl.multiple_of(owner * rows, rows), rows), :]
    squares_ref[...] = jnp.broadcast_to(squares[None], squares_ref.shape)


def finish(mine, arrived, at, weight):
    half = mine[0].shape[0]
    block = jax.ShapeDtypeStruct((2 * half // DP, LANE), F32)
    return call(
        finish_kernel,
        (block,) * DP + (jax.ShapeDtypeStruct((Z * CORE, 1, LANE), F32),),
        [pl.BlockSpec(memory_space=pltpu.SMEM)] + [whole()] * 4,
        (whole(),) * (DP + 1),
        scalars=1,
        scratch=[VMEM((2 * half, LANE), F32)],
        flops=4 * arrived[0].size,
        moved=4 * arrived[0].size,
    )(at, weight, *mine, *arrived)


def pass_kernel(in_ref, out_ref):
    out_ref[...] = jnp.broadcast_to(jnp.sum(in_ref[...], axis=0, keepdims=True), out_ref.shape)


def keep_kernel(in_ref, out_ref):
    out_ref[...] = in_ref[...]


def keep(value):
    return call(keep_kernel, jax.ShapeDtypeStruct(value.shape, value.dtype), [whole()], whole())(value)


def combine_kernel(clip_bound, at_ref, squares_ref, *refs):
    blocks, out_ref = refs[:DP], refs[DP]
    total = None
    for k in range(DP):
        example = jnp.bitwise_and(at_ref[3] + DP - k, DP - 1)
        squares = jnp.sum(squares_ref[pl.ds(example * X, X)])
        factor = jnp.minimum(1.0, clip_bound * lax.rsqrt(jnp.full((1, LANE), squares, F32) + 1e-06))
        term = blocks[k][...] * factor
        total = term if total is None else total + term
    out_ref[...] = total.T


def turn(n, k):
    return [(i, (i + k) % n) for i in range(n)]


def exchanged(value, axis):
    return lax.all_to_all(value, axis, split_axis=0, concat_axis=0, tiled=True)


def per_device(hidden, norm_gain, cotangent, loss_weight):
    hidden, cot = hidden[0], cotangent[0]
    tokens, features = hidden.shape
    outs = cot.shape[1]
    doc_length = tokens * X * Z * CORE
    at = jnp.stack([lax.axis_index(n).astype(jnp.int32) for n in ("x", "z", "core", "dp")])
    swap = functools.partial(lax.ppermute, axis_name="core", perm=turn(CORE, 1))
    gain = norm_gain.reshape(features // LANE, LANE)
    weight = loss_weight * (1.0 / math.sqrt(doc_length))
    hidden, gain, weight, at, cto = lax.optimization_barrier((hidden, gain, weight, at, cot.T))
    ctp = swap(cto)
    own, par = [], []
    for half in range(HALVES):
        kept, sent = prep(half, hidden, gain, at)
        own.append(kept)
        par.append(swap(sent))

    def block(k):
        return product(k, own, par, cto, ctp, at)

    blocks = {k: block(k) for k in (2, 1, 3, 0)}
    mine, summed = [], []
    for chunk in range(2):
        arrived = [lax.ppermute(blocks[k][chunk], "x", turn(X, k)) for k in (2, 1, 3)]
        ready, kept = gather(blocks[0][chunk], *arrived, at)
        mine.append(kept)
        summed.append(exchanged(ready, "z"))
    *tiles, squares = finish(mine, summed, at, weight)
    arrived = [tiles[0]] + [lax.ppermute(tiles[k], "dp", turn(DP, k)) for k in range(1, DP)]
    arrived[0] = keep(arrived[0])
    squares = exchanged(squares, ("z", "core"))
    squares = call(pass_kernel, jax.ShapeDtypeStruct((DP * X, 1, LANE), F32), [whole()], whole())(squares)
    squares = exchanged(squares, ("dp", "x"))
    clip_bound = math.sqrt(features * outs)
    return call(
        functools.partial(combine_kernel, clip_bound),
        jax.ShapeDtypeStruct((LANE, outs // DP), F32),
        [whole()] * (DP + 1),
        whole(),
        scalars=1,
    )(at, squares, *arrived)


def solution(mesh):
    fine = Mesh(mesh.devices.reshape(DP, X, Z, CORE), ("dp", "x", "z", "core"))
    ctx = ("x", "z", "core")
    in_specs = (P("dp", ctx, None), P(), P("dp", ctx, None), P("dp"))
    out_specs = P(ctx, "dp")
    return jax.shard_map(
        per_device, mesh=fine, in_specs=in_specs, out_specs=out_specs, check_vma=False
    )
```

time: 258 us -> 137 us (0.53)
  waiting for transfers between devices: 190 us -> 51 us
  starting transfers between devices: 0.01 us -> 26.5 us
  Pallas kernels: 0 us -> 17.6 us
  between operations: 14.8 us -> 0.76 us
  matrix products: 13 us -> 0 us
  other arithmetic: 9.02 us -> 0.08 us
  local copies, waits for them, and re-layouts: 0.67 us -> 5.39 us
  blocking collectives: 30.3 us -> 34.9 us
    reduce_scatter x1 -> x0, waiting for transfers between devices: 190 us -> none  [per_device(): lax.psum_scatter(weight * lax.dot_general(normed, upstream, contract, pre...]
    ppermute x0 -> x12, waiting for transfers between devices: none -> 44.7 us  [the longest x6 40.3 us: per_device(): lax.ppermute(blocks[k][chunk], 'x', turn(X, k))]
    pallas_call x0 -> x12, Pallas kernels: none -> 17.6 us  [the longest x4 7.24 us: product(): call(functools.partial(product_kernel, turns), (shape, shape), [whole()]...]
    ppermute x0 -> x12, starting transfers between devices: none -> 14.8 us  [the longest x6 5.86 us: per_device(): lax.ppermute(blocks[k][chunk], 'x', turn(X, k))]
    dot_general x1 -> x0, matrix products: 13 us -> none  [per_device(): lax.dot_general(normed, upstream, contract, preferred_element_type=jnp.fl...]
    all_to_all x0 -> x2, starting transfers between devices: none -> 11.7 us  [exchanged(): return lax.all_to_all(value, axis, split_axis=0, concat_axis=0, tiled=True)]
    reduce_sum x4 -> x0, other arithmetic: 8.04 us -> none  [the longest x1 5.1 us: per_device(): jnp.mean(widened * widened, axis=1, keepdims=True) + 1e-05]
    all_to_all x0 -> x2, waiting for transfers between devices: none -> 6.28 us  [exchanged(): return lax.all_to_all(value, axis, split_axis=0, concat_axis=0, tiled=True)]
  transfers between devices with their start and end apart: 1 -> 14, of which waited for: 1 -> 8; matrix products, arithmetic and copies ran while one was open for 0% -> 0% of each run, Pallas kernels for 0% -> 7%
where the time goes in v2:
time: 137 us; the launch traced here: 136 us
  waiting for transfers between devices  51 us (37%)
  blocking collectives  34.9 us (25%)
  starting transfers between devices  26.5 us (19%)
  Pallas kernels  17.6 us (13%)
  local copies, waits for them, and re-layouts  5.39 us (4%)
    ppermute x6, waiting for transfers between devices, per_device(): lax.ppermute(blocks[k][chunk], 'x', turn(X, k))  40.3 us
    all_to_all x2, blocking collectives, exchanged(): return lax.all_to_all(value, axis, split_axis=0, concat_axis=0, tiled=True)  34.9 us
    all_to_all x2, starting transfers between devices, exchanged(): return lax.all_to_all(value, axis, split_axis=0, concat_axis=0, tiled=True)  11.7 us
    pallas_call x4, Pallas kernels, product(): call(functools.partial(product_kernel, turns), (shape, shape), [whole()]...  7.24 us
    all_to_all x2, waiting for transfers between devices, exchanged(): return lax.all_to_all(value, axis, split_axis=0, concat_axis=0, tiled=True)  6.28 us
    ppermute x6, starting transfers between devices, per_device(): lax.ppermute(blocks[k][chunk], 'x', turn(X, k))  5.86 us
    unnamed x5, local copies, waits for them, and re-layouts  5.39 us
    pallas_call x2, Pallas kernels, prep(): call(functools.partial(prep_kernel, half), (part, part), [whole(), whole(...  5.11 us
  transfers between devices with their start and end apart: 14, of which 8 were waited for; matrix products, arithmetic and copies ran while one was open for 0% of the time, Pallas kernels for 7%

profile of v2, /device:TPU:1, one launch (start us, length us, event | category | flops | bytes accessed | tf_op | source)
XLA Modules:
  0.0 136.2 jit_solution(14769314258835268753)
XLA Ops:
  0.7 1.3 copy.5
  1.9 0.1 pad_add_fusion.at_ref
  2.0 0.0 copy-start
  2.0 3.4 %copy-done = bf16[1,512,8192]{2,1,0:T(8,128)(2,1)S(1)} copy-done((bf16[1,512,8192]{2,1,0:T(8,128)(2,1)S(1)}, bf16[1,512,8192]{2,1,0:T(8,128)(2,1)}, u32[]{:S(2)}) %copy-start) | copy-done | bytes 8388632
  5.4 0.0 copy-start.1
  5.4 0.8 copy-done.1
  6.1 2.6 %shard_map.47 = (bf16[256,4096]{1,0:T(8,128)(2,1)S(1)}, bf16[256,4096]{1,0:T(8,128)(2,1)S(1)}) custom-call(s32[4]{0:T(128)S(1)} %pad_add_fusion.at_ref, bf16[512,8192]{1,0:T(8,128)(2,1)S(1)} %bitcast.9, f32[64,128]{1,0:T(8,128)S(1)} %bitcast.16), custom_call_target="tpu_custom_call" | custom-call | flops 8388608 | bytes 8388608 | tf_op jit(solution)/shard_map/pallas_call | solution.py:67
  8.7 3.3 %collective-permute-start.1 = (bf16[256,4096]{1,0:T(8,128)(2,1)S(1)}, bf16[256,4096]{1,0:T(8,128)(2,1)S(1)}, u32[]{:S(2)}, u32[]{:S(2)}) collective-permute-start(bf16[256,4096]{1,0:T(8,128)(2,1)S(1)} %get-tuple-element.38), channel_id=1, source_target_pairs={{0,1},{1,0},{2,3},{3,2},{4,5},{5,4},{6,7},{7,6},{8,9},{9,8},{10,11... | collective-permute-start | bytes 6291464 | tf_op jit(solution)/shard_map/ppermute | solution.py:226
  12.0 2.6 %shard_map.46 = (bf16[256,4096]{1,0:T(8,128)(2,1)S(1)}, bf16[256,4096]{1,0:T(8,128)(2,1)S(1)}) custom-call(s32[4]{0:T(128)S(1)} %pad_add_fusion.at_ref, bf16[512,8192]{1,0:T(8,128)(2,1)S(1)} %bitcast.10, f32[64,128]{1,0:T(8,128)S(1)} %bitcast.17), custom_call_target="tpu_custom_call" | custom-call | flops 8388608 | bytes 8388608 | tf_op jit(solution)/shard_map/pallas_call | solution.py:67
  14.5 0.1 collective-permute-start
  14.6 0.5 collective-permute-start.2
  15.1 4.4 %collective-permute-done.2.refs_5_ = bf16[512,512]{1,0:T(8,128)(2,1)S(1)} collective-permute-done((bf16[512,512]{1,0:T(8,128)(2,1)S(1)}, bf16[512,512]{1,0:T(8,128)(2,1)S(1)}, u32[]{:S(2)}, u32[]{:S(2)}) %collective-permute-start.2) | collective-permute-done | bytes 524320 | tf_op jit(solution)/shard_map/ppermute | solution.py:221
  19.5 0.0 collective-permute-done.1.refs_3_
  19.5 0.0 collective-permute-done.refs_2_
  19.5 1.8 %shard_map.51 = (bf16[2048,128]{1,0:T(8,128)(2,1)S(1)}, bf16[2048,128]{1,0:T(8,128)(2,1)S(1)}) custom-call(s32[4]{0:T(128)S(1)} %pad_add_fusion.at_ref, bf16[256,4096]{1,0:T(8,128)(2,1)S(1)} %get-tuple-element.35.refs_0_, bf16[256,4096]{1,0:T(8,128)(2,1)S(1)} %get-tuple-element.36.refs_1_, bf16[256,4096]{1,0:T(8,128)(2,1)S(1)} %collective-permute-done.refs_2_, ...), custom_call_target="tpu_custom_call" | custom-call | flops 1073741824 | bytes 4194304 | tf_op jit(solution)/shard_map/pallas_call | solution.py:104
  21.4 0.9 collective-permute-start.5
  22.2 1.8 %shard_map.50 = (bf16[2048,128]{1,0:T(8,128)(2,1)S(1)}, bf16[2048,128]{1,0:T(8,128)(2,1)S(1)}) custom-call(s32[4]{0:T(128)S(1)} %pad_add_fusion.at_ref, bf16[256,4096]{1,0:T(8,128)(2,1)S(1)} %get-tuple-element.35.refs_0_, bf16[256,4096]{1,0:T(8,128)(2,1)S(1)} %get-tuple-element.36.refs_1_, bf16[256,4096]{1,0:T(8,128)(2,1)S(1)} %collective-permute-done.refs_2_, ...), custom_call_target="tpu_custom_call" | custom-call | flops 1073741824 | bytes 4194304 | tf_op jit(solution)/shard_map/pallas_call | solution.py:104
  24.0 0.8 collective-permute-start.4
  24.8 1.8 %shard_map.49 = (bf16[2048,128]{1,0:T(8,128)(2,1)S(1)}, bf16[2048,128]{1,0:T(8,128)(2,1)S(1)}) custom-call(s32[4]{0:T(128)S(1)} %pad_add_fusion.at_ref, bf16[256,4096]{1,0:T(8,128)(2,1)S(1)} %get-tuple-element.35.refs_0_, bf16[256,4096]{1,0:T(8,128)(2,1)S(1)} %get-tuple-element.36.refs_1_, bf16[256,4096]{1,0:T(8,128)(2,1)S(1)} %collective-permute-done.refs_2_, ...), custom_call_target="tpu_custom_call" | custom-call | flops 1073741824 | bytes 4194304 | tf_op jit(solution)/shard_map/pallas_call | solution.py:104
  26.6 1.3 collective-permute-start.3
  27.9 1.8 %shard_map.48 = (f32[2048,128]{1,0:T(8,128)S(1)}, f32[2048,128]{1,0:T(8,128)S(1)}) custom-call(s32[4]{0:T(128)S(1)} %pad_add_fusion.at_ref, bf16[256,4096]{1,0:T(8,128)(2,1)S(1)} %get-tuple-element.35.refs_0_, bf16[256,4096]{1,0:T(8,128)(2,1)S(1)} %get-tuple-element.36.refs_1_, bf16[256,4096]{1,0:T(8,128)(2,1)S(1)} %collective-permute-done.refs_2_, ...), custom_call_target="tpu_custom_call" | custom-call | flops 1073741824 | bytes 4194304 | tf_op jit(solution)/shard_map/pallas_call | solution.py:104
  29.7 4.8 %collective-permute-done.5.r3_ref = bf16[2048,128]{1,0:T(8,128)(2,1)S(1)} collective-permute-done((bf16[2048,128]{1,0:T(8,128)(2,1)S(1)}, bf16[2048,128]{1,0:T(8,128)(2,1)S(1)}, u32[]{:S(2)}, u32[]{:S(2)}) %collective-permute-start.5) | collective-permute-done | bytes 524320 | tf_op jit(solution)/shard_map/ppermute | solution.py:234
  34.6 4.6 %collective-permute-done.4.r2_ref = bf16[2048,128]{1,0:T(8,128)(2,1)S(1)} collective-permute-done((bf16[2048,128]{1,0:T(8,128)(2,1)S(1)}, bf16[2048,128]{1,0:T(8,128)(2,1)S(1)}, u32[]{:S(2)}, u32[]{:S(2)}) %collective-permute-start.4) | collective-permute-done | bytes 524320 | tf_op jit(solution)/shard_map/ppermute | solution.py:234
  39.1 9.4 %collective-permute-done.3.r1_ref = bf16[2048,128]{1,0:T(8,128)(2,1)S(1)} collective-permute-done((bf16[2048,128]{1,0:T(8,128)(2,1)S(1)}, bf16[2048,128]{1,0:T(8,128)(2,1)S(1)}, u32[]{:S(2)}, u32[]{:S(2)}) %collective-permute-start.3) | collective-permute-done | bytes 524320 | tf_op jit(solution)/shard_map/ppermute | solution.py:234
  48.5 1.6 %shard_map.52 = (bf16[8,256,128]{2,1,0:T(8,128)(2,1)}, f32[256,128]{1,0:T(8,128)S(1)}) custom-call(s32[4]{0:T(128)S(1)} %pad_add_fusion.at_ref, f32[2048,128]{1,0:T(8,128)S(1)} %get-tuple-element.40.own_ref, bf16[2048,128]{1,0:T(8,128)(2,1)S(1)} %collective-permute-done.3.r1_ref, bf16[2048,128]{1,0:T(8,128)(2,1)S(1)} %collective-permute-done.4.r2_ref, ...), custom_call_target="tpu_custom_call" | custom-call | flops 1048576 | bytes 3145728 | tf_op jit(solution)/shard_map/pallas_call | solution.py:132
  50.1 8.2 %all-to-all-start = ((bf16[8,256,128]{2,1,0:T(8,128)(2,1)}), bf16[8,256,128]{2,1,0:T(8,128)(2,1)S(1)}, u32[]{:S(2)}, u32[]{:S(2)}) async-start(bf16[8,256,128]{2,1,0:T(8,128)(2,1)} %get-tuple-element.50), calls=%async_computation | async-start | bytes 1048576 | tf_op jit(solution)/shard_map/all_to_all | solution.py:208
  58.3 0.0 collective-permute-start.8
  58.3 1.5 %collective-permute-start.7 = (bf16[2048,128]{1,0:T(8,128)(2,1)S(1)}, bf16[2048,128]{1,0:T(8,128)(2,1)S(1)}, u32[]{:S(2)}, u32[]{:S(2)}) collective-permute-start(bf16[2048,128]{1,0:T(8,128)(2,1)S(1)} %get-tuple-element.47), channel_id=1, source_target_pairs={{0,16},{16,32},{32,48},{48,0},{1,17},{17,33},{33,49},{49,1},{2,18}... | collective-permute-start | bytes 1572872 | tf_op jit(solution)/shard_map/ppermute | solution.py:234
  59.7 1.5 %collective-permute-start.6 = (bf16[2048,128]{1,0:T(8,128)(2,1)S(1)}, bf16[2048,128]{1,0:T(8,128)(2,1)S(1)}, u32[]{:S(2)}, u32[]{:S(2)}) collective-permute-start(bf16[2048,128]{1,0:T(8,128)(2,1)S(1)} %get-tuple-element.46), channel_id=1, source_target_pairs={{0,32},{16,48},{32,0},{48,16},{1,33},{17,49},{33,1},{49,17},{2,34}... | collective-permute-start | bytes 1572872 | tf_op jit(solution)/shard_map/ppermute | solution.py:234
  61.2 7.9 %collective-permute-done.8.r3_ref = bf16[2048,128]{1,0:T(8,128)(2,1)S(1)} collective-permute-done((bf16[2048,128]{1,0:T(8,128)(2,1)S(1)}, bf16[2048,128]{1,0:T(8,128)(2,1)S(1)}, u32[]{:S(2)}, u32[]{:S(2)}) %collective-permute-start.8) | collective-permute-done | bytes 524320 | tf_op jit(solution)/shard_map/ppermute | solution.py:234
  69.1 1.3 collective-permute-done.7.r2_ref
  70.4 12.3 %collective-permute-done.6.r1_ref = bf16[2048,128]{1,0:T(8,128)(2,1)S(1)} collective-permute-done((bf16[2048,128]{1,0:T(8,128)(2,1)S(1)}, bf16[2048,128]{1,0:T(8,128)(2,1)S(1)}, u32[]{:S(2)}, u32[]{:S(2)}) %collective-permute-start.6) | collective-permute-done | bytes 524320 | tf_op jit(solution)/shard_map/ppermute | solution.py:234
  82.7 0.8 shard_map.53
  83.6 0.0 all-to-all-done.refs_2_
  83.6 19.8 %all_to_all.20.refs_3_ = bf16[8,256,128]{2,1,0:T(8,128)(2,1)S(1)} all-to-all(bf16[8,256,128]{2,1,0:T(8,128)(2,1)S(1)} %get-tuple-element.51), channel_id=1, replica_groups=mesh['dp'=4,'x'=4,'z'=8,'core'=2] {'z'}, dimensions={0} | all-to-all | bytes 1048576 | tf_op jit(solution)/shard_map/all_to_all | solution.py:208
  103.3 0.8 shard_map.54
  104.2 1.4 %collective-permute-start.9 = (f32[128,128]{1,0:T(8,128)S(1)}, f32[128,128]{1,0:T(8,128)S(1)}, u32[]{:S(2)}, u32[]{:S(2)}) collective-permute-start(f32[128,128]{1,0:T(8,128)S(1)} %get-tuple-element.54), channel_id=1, source_target_pairs={{0,64},{64,128},{128,192},{192,0},{1,65},{65,129},{129,193},{193,1... | collective-permute-start | bytes 196616 | tf_op jit(solution)/shard_map/ppermute | solution.py:239
  105.5 2.6 %collective-permute-start.10 = (f32[128,128]{1,0:T(8,128)S(1)}, f32[128,128]{1,0:T(8,128)S(1)}, u32[]{:S(2)}, u32[]{:S(2)}) collective-permute-start(f32[128,128]{1,0:T(8,128)S(1)} %get-tuple-element.55), channel_id=1, source_target_pairs={{0,128},{64,192},{128,0},{192,64},{1,129},{65,193},{129,1},{193,65... | collective-permute-start | bytes 196616 | tf_op jit(solution)/shard_map/ppermute | solution.py:239
  108.2 1.1 collective-permute-start.11
  109.2 15.1 %all_to_all.21.in_ref = f32[16,1,128]{2,1,0:T(1,128)S(1)} all-to-all(f32[16,1,128]{2,1,0:T(1,128)S(1)} %get-tuple-element.52), channel_id=1, replica_groups=mesh['dp'=4,'x'=4,'z'=8,'core'=2] {'z','core'}, dimensions={0} | all-to-all | bytes 16384 | tf_op jit(solution)/shard_map/all_to_all | solution.py:208
  124.4 0.6 shard_map.55
  125.0 3.5 %all-to-all-start.3 = ((f32[16,1,128]{2,1,0:T(1,128)}), f32[16,1,128]{2,1,0:T(1,128)S(1)}, u32[]{:S(2)}, u32[]{:S(2)}) async-start(f32[16,1,128]{2,1,0:T(1,128)} %shard_map.55), calls=%async_computation.3 | async-start | bytes 16384 | tf_op jit(solution)/shard_map/all_to_all | solution.py:208
  128.5 6.3 %all-to-all-done.3.squares_ref = f32[16,1,128]{2,1,0:T(1,128)S(1)} async-done(((f32[16,1,128]{2,1,0:T(1,128)}), f32[16,1,128]{2,1,0:T(1,128)S(1)}, u32[]{:S(2)}, u32[]{:S(2)}) %all-to-all-start.3) | async-done | bytes 8224 | tf_op jit(solution)/shard_map/all_to_all | solution.py:208
  134.8 0.0 collective-permute-done.9.refs_1_
  134.8 0.0 collective-permute-done.10.refs_2_
  134.8 0.0 collective-permute-done.11.refs_3_
  134.8 1.4 %shard_map.57 = f32[128,128]{1,0:T(8,128)} custom-call(s32[4]{0:T(128)S(1)} %pad_add_fusion.at_ref, f32[16,1,128]{2,1,0:T(1,128)S(1)} %all-to-all-done.3.squares_ref, f32[128,128]{1,0:T(8,128)S(1)} %shard_map.56.refs_0_, f32[128,128]{1,0:T(8,128)S(1)} %collective-permute-done.9.refs_1_, f32[128,128]{1,0:T(8,128)S(1)} %collective-permute-done.10.refs_2_, ...), custom_call_target="tpu_custom_call" | custom-call | tf_op jit(solution)/shard_map/pallas_call | solution.py:245
  (1 shorter events, 0.0 us)
Async XLA Ops:
  2.0 3.4 %copy-start = (bf16[1,512,8192]{2,1,0:T(8,128)(2,1)S(1)}, bf16[1,512,8192]{2,1,0:T(8,128)(2,1)}, u32[]{:S(2)}) copy-start(bf16[1,512,8192]{2,1,0:T(8,128)(2,1)} %param.4) | copy-start | bytes 25165828
  5.4 0.8 copy-start.1
  8.7 10.8 %collective-permute-start.1 = (bf16[256,4096]{1,0:T(8,128)(2,1)S(1)}, bf16[256,4096]{1,0:T(8,128)(2,1)S(1)}, u32[]{:S(2)}, u32[]{:S(2)}) collective-permute-start(bf16[256,4096]{1,0:T(8,128)(2,1)S(1)} %get-tuple-element.38), channel_id=1, source_target_pairs={{0,1},{1,0},{2,3},{3,2},{4,5},{5,4},{6,7},{7,6},{8,9},{9,8},{10,11... | collective-permute-start | bytes 6291464 | tf_op jit(solution)/shard_map/ppermute | solution.py:226
  14.5 5.0 %collective-permute-start = (bf16[256,4096]{1,0:T(8,128)(2,1)S(1)}, bf16[256,4096]{1,0:T(8,128)(2,1)S(1)}, u32[]{:S(2)}, u32[]{:S(2)}) collective-permute-start(bf16[256,4096]{1,0:T(8,128)(2,1)S(1)} %get-tuple-element.37), channel_id=1, source_target_pairs={{0,1},{1,0},{2,3},{3,2},{4,5},{5,4},{6,7},{7,6},{8,9},{9,8},{10,11... | collective-permute-start | bytes 6291464 | tf_op jit(solution)/shard_map/ppermute | solution.py:226
  14.6 4.9 %collective-permute-start.2 = (bf16[512,512]{1,0:T(8,128)(2,1)S(1)}, bf16[512,512]{1,0:T(8,128)(2,1)S(1)}, u32[]{:S(2)}, u32[]{:S(2)}) collective-permute-start(bf16[512,512]{1,0:T(8,128)(2,1)S(1)} %bitcast.11), channel_id=1, source_target_pairs={{0,1},{1,0},{2,3},{3,2},{4,5},{5,4},{6,7},{7,6},{8,9},{9,8},{10,11... | collective-permute-start | bytes 1572872 | tf_op jit(solution)/shard_map/ppermute | solution.py:221
  21.4 13.2 %collective-permute-start.5 = (bf16[2048,128]{1,0:T(8,128)(2,1)S(1)}, bf16[2048,128]{1,0:T(8,128)(2,1)S(1)}, u32[]{:S(2)}, u32[]{:S(2)}) collective-permute-start(bf16[2048,128]{1,0:T(8,128)(2,1)S(1)} %get-tuple-element.43), channel_id=1, source_target_pairs={{0,48},{16,0},{32,16},{48,32},{1,49},{17,1},{33,17},{49,33},{2,50}... | collective-permute-start | bytes 1572872 | tf_op jit(solution)/shard_map/ppermute | solution.py:234
  24.0 15.1 %collective-permute-start.4 = (bf16[2048,128]{1,0:T(8,128)(2,1)S(1)}, bf16[2048,128]{1,0:T(8,128)(2,1)S(1)}, u32[]{:S(2)}, u32[]{:S(2)}) collective-permute-start(bf16[2048,128]{1,0:T(8,128)(2,1)S(1)} %get-tuple-element.42), channel_id=1, source_target_pairs={{0,16},{16,32},{32,48},{48,0},{1,17},{17,33},{33,49},{49,1},{2,18}... | collective-permute-start | bytes 1572872 | tf_op jit(solution)/shard_map/ppermute | solution.py:234
  26.6 21.9 %collective-permute-start.3 = (bf16[2048,128]{1,0:T(8,128)(2,1)S(1)}, bf16[2048,128]{1,0:T(8,128)(2,1)S(1)}, u32[]{:S(2)}, u32[]{:S(2)}) collective-permute-start(bf16[2048,128]{1,0:T(8,128)(2,1)S(1)} %get-tuple-element.41), channel_id=1, source_target_pairs={{0,32},{16,48},{32,0},{48,16},{1,33},{17,49},{33,1},{49,17},{2,34}... | collective-permute-start | bytes 1572872 | tf_op jit(solution)/shard_map/ppermute | solution.py:234
  50.1 33.5 %all-to-all-start = ((bf16[8,256,128]{2,1,0:T(8,128)(2,1)}), bf16[8,256,128]{2,1,0:T(8,128)(2,1)S(1)}, u32[]{:S(2)}, u32[]{:S(2)}) async-start(bf16[8,256,128]{2,1,0:T(8,128)(2,1)} %get-tuple-element.50), calls=%async_computation | async-start | bytes 1048576 | tf_op jit(solution)/shard_map/all_to_all | solution.py:208
  58.3 10.8 %collective-permute-start.8 = (bf16[2048,128]{1,0:T(8,128)(2,1)S(1)}, bf16[2048,128]{1,0:T(8,128)(2,1)S(1)}, u32[]{:S(2)}, u32[]{:S(2)}) collective-permute-start(bf16[2048,128]{1,0:T(8,128)(2,1)S(1)} %get-tuple-element.48), channel_id=1, source_target_pairs={{0,48},{16,0},{32,16},{48,32},{1,49},{17,1},{33,17},{49,33},{2,50}... | collective-permute-start | bytes 1572872 | tf_op jit(solution)/shard_map/ppermute | solution.py:234
  58.3 12.1 %collective-permute-start.7 = (bf16[2048,128]{1,0:T(8,128)(2,1)S(1)}, bf16[2048,128]{1,0:T(8,128)(2,1)S(1)}, u32[]{:S(2)}, u32[]{:S(2)}) collective-permute-start(bf16[2048,128]{1,0:T(8,128)(2,1)S(1)} %get-tuple-element.47), channel_id=1, source_target_pairs={{0,16},{16,32},{32,48},{48,0},{1,17},{17,33},{33,49},{49,1},{2,18}... | collective-permute-start | bytes 1572872 | tf_op jit(solution)/shard_map/ppermute | solution.py:234
  59.7 23.0 %collective-permute-start.6 = (bf16[2048,128]{1,0:T(8,128)(2,1)S(1)}, bf16[2048,128]{1,0:T(8,128)(2,1)S(1)}, u32[]{:S(2)}, u32[]{:S(2)}) collective-permute-start(bf16[2048,128]{1,0:T(8,128)(2,1)S(1)} %get-tuple-element.46), channel_id=1, source_target_pairs={{0,32},{16,48},{32,0},{48,16},{1,33},{17,49},{33,1},{49,17},{2,34}... | collective-permute-start | bytes 1572872 | tf_op jit(solution)/shard_map/ppermute | solution.py:234
  104.2 30.6 %collective-permute-start.9 = (f32[128,128]{1,0:T(8,128)S(1)}, f32[128,128]{1,0:T(8,128)S(1)}, u32[]{:S(2)}, u32[]{:S(2)}) collective-permute-start(f32[128,128]{1,0:T(8,128)S(1)} %get-tuple-element.54), channel_id=1, source_target_pairs={{0,64},{64,128},{128,192},{192,0},{1,65},{65,129},{129,193},{193,1... | collective-permute-start | bytes 196616 | tf_op jit(solution)/shard_map/ppermute | solution.py:239
  105.5 29.2 %collective-permute-start.10 = (f32[128,128]{1,0:T(8,128)S(1)}, f32[128,128]{1,0:T(8,128)S(1)}, u32[]{:S(2)}, u32[]{:S(2)}) collective-permute-start(f32[128,128]{1,0:T(8,128)S(1)} %get-tuple-element.55), channel_id=1, source_target_pairs={{0,128},{64,192},{128,0},{192,64},{1,129},{65,193},{129,1},{193,65... | collective-permute-start | bytes 196616 | tf_op jit(solution)/shard_map/ppermute | solution.py:239
  108.2 26.6 %collective-permute-start.11 = (f32[128,128]{1,0:T(8,128)S(1)}, f32[128,128]{1,0:T(8,128)S(1)}, u32[]{:S(2)}, u32[]{:S(2)}) collective-permute-start(f32[128,128]{1,0:T(8,128)S(1)} %get-tuple-element.56), channel_id=1, source_target_pairs={{0,192},{64,0},{128,64},{192,128},{1,193},{65,1},{129,65},{193,129... | collective-permute-start | bytes 196616 | tf_op jit(solution)/shard_map/ppermute | solution.py:239
  125.0 9.8 %all-to-all-start.3 = ((f32[16,1,128]{2,1,0:T(1,128)}), f32[16,1,128]{2,1,0:T(1,128)S(1)}, u32[]{:S(2)}, u32[]{:S(2)}) async-start(f32[16,1,128]{2,1,0:T(1,128)} %shard_map.55), calls=%async_computation.3 | async-start | bytes 16384 | tf_op jit(solution)/shard_map/all_to_all | solution.py:208

commit v3 on v2

--- a/solution.py
+++ b/solution.py
@@ -76,36 +76,42 @@
     )(at, hidden, gain)
 
 
-def product_kernel(turns, at_ref, *refs):
+def turn_kernel(in_ref, out_ref):
+    out_ref[...] = in_ref[...].T
+
+
+def turned(value):
+    return call(turn_kernel, jax.ShapeDtypeStruct(value.shape[::-1], value.dtype), [whole()], whole())(value)
+
+
+def product_kernel(turns, chunk, at_ref, *refs):
     owner = jnp.bitwise_and(at_ref[0] + turns, X - 1)
     tokens = refs[: 2 * HALVES]
     cot_refs = refs[2 * HALVES : 2 * HALVES + 2]
-    outs = refs[2 * HALVES + 2 :]
+    out_ref = refs[2 * HALVES + 2]
     half = cot_refs[0].shape[0] // 2
     rows = tokens[0].shape[0]
     for p in range(Z // 2):
         lanes = pl.ds(pl.multiple_of(owner * (Z * LANE) + p * 2 * LANE, 2 * LANE), 2 * LANE)
         total = None
         for n, t in enumerate(tokens):
-            c = cot_refs[n // HALVES][:, (n % HALVES) * rows : (n % HALVES + 1) * rows]
+            c = cot_refs[n // HALVES]
+            c = c[chunk * half : (chunk + 1) * half, (n % HALVES) * rows : (n % HALVES + 1) * rows]
             term = jnp.dot(c, t[:, lanes], preferred_element_type=F32)
             total = term if total is None else total + term
         for i in range(2):
             at = slice((2 * p + i) * half, (2 * p + i + 1) * half)
-            tile = total[:, i * LANE : (i + 1) * LANE]
-            outs[0][at, :] = tile[:half].astype(outs[0].dtype)
-            outs[1][at, :] = tile[half:].astype(outs[1].dtype)
-
-
-def product(turns, own, par, cto, ctp, at):
-    outs = cto.shape[0]
+            out_ref[at, :] = total[:, i * LANE : (i + 1) * LANE].astype(out_ref.dtype)
+
+
+def product(turns, chunk, own, par, cto, ctp, at):
+    outs = cto.shape[0] // 2
     tokens = 2 * cto.shape[1]
-    shape = jax.ShapeDtypeStruct((Z * outs // 2, LANE), WIRE if turns else F32)
-    return call(
-        functools.partial(product_kernel, turns),
-        (shape, shape),
+    return call(
+        functools.partial(product_kernel, turns, chunk),
+        jax.ShapeDtypeStruct((Z * outs, LANE), WIRE if turns else F32),
         [whole()] * (2 * HALVES + 2),
-        (whole(), whole()),
+        whole(),
         scalars=1,
         flops=2 * outs * tokens * Z * LANE,
         moved=4 * tokens * Z * LANE,
@@ -140,40 +146,58 @@
     )(at, own, r1, r2, r3)
 
 
-def finish_kernel(at_ref, weight_ref, *refs):
-    mine, arrived, outs = refs[:2], refs[2:4], refs[4 : 4 + DP]
-    squares_ref, tile = refs[4 + DP :]
-    half = mine[0].shape[0]
-    weight = weight_ref[0]
-    squares = jnp.zeros((1, LANE), F32)
-    for n in range(2):
-        total = mine[n][...]
-        for j in range(Z):
-            other = jnp.where(at_ref[1] == j, 0.0, 1.0)
-            total = total + arrived[n][j].astype(F32) * other
-        total = total * weight
-        tile[n * half : (n + 1) * half, :] = total
-        squares = squares + jnp.sum(total * total, axis=0, keepdims=True)
+def finished(at_ref, weight_ref, mine_ref, arrived_ref):
+    total = mine_ref[...]
+    for j in range(Z):
+        total = total + arrived_ref[j].astype(F32) * jnp.where(at_ref[1] == j, 0.0, 1.0)
+    total = total * weight_ref[0]
+    return total, jnp.sum(total * total, axis=0, keepdims=True)
+
+
+def first_kernel(at_ref, weight_ref, mine_ref, arrived_ref, tile_ref, squares_ref):
+    total, squares = finished(at_ref, weight_ref, mine_ref, arrived_ref)
+    tile_ref[...] = total
+    squares_ref[...] = jnp.broadcast_to(squares, squares_ref.shape)
+
+
+def first(mine, arrived, at, weight):
+    return call(
+        first_kernel,
+        (jax.ShapeDtypeStruct(mine.shape, F32), jax.ShapeDtypeStruct((8, LANE), F32)),
+        [pl.BlockSpec(memory_space=pltpu.SMEM)] + [whole()] * 2,
+        (whole(), whole()),
+        scalars=1,
+        flops=4 * arrived.size,
+        moved=4 * arrived.size,
+    )(at, weight, mine, arrived)
+
+
+def last_kernel(at_ref, weight_ref, mine_ref, arrived_ref, before_ref, partial_ref, *refs):
+    outs, squares_ref, tile = refs[:DP], refs[DP], refs[DP + 1]
+    total, squares = finished(at_ref, weight_ref, mine_ref, arrived_ref)
+    half = total.shape[0]
+    squares_ref[...] = jnp.broadcast_to((squares + partial_ref[:1, :])[None], squares_ref.shape)
+    tile[:half, :] = before_ref[...]
+    tile[half:, :] = total
     rows = 2 * half // DP
     for k in range(DP):
         owner = jnp.bitwise_and(at_ref[3] + k, DP - 1)
         outs[k][...] = tile[pl.ds(pl.multiple_of(owner * rows, rows), rows), :]
-    squares_ref[...] = jnp.broadcast_to(squares[None], squares_ref.shape)
-
-
-def finish(mine, arrived, at, weight):
-    half = mine[0].shape[0]
+
+
+def last(mine, arrived, before, partial, at, weight):
+    half = mine.shape[0]
     block = jax.ShapeDtypeStruct((2 * half // DP, LANE), F32)
     return call(
-        finish_kernel,
+        last_kernel,
         (block,) * DP + (jax.ShapeDtypeStruct((Z * CORE, 1, LANE), F32),),
         [pl.BlockSpec(memory_space=pltpu.SMEM)] + [whole()] * 4,
         (whole(),) * (DP + 1),
         scalars=1,
         scratch=[VMEM((2 * half, LANE), F32)],
-        flops=4 * arrived[0].size,
-        moved=4 * arrived[0].size,
-    )(at, weight, *mine, *arrived)
+        flops=4 * arrived.size,
+        moved=4 * arrived.size,
+    )(at, weight, mine, arrived, before, partial)
 
 
 def pass_kernel(in_ref, out_ref):
@@ -188,16 +212,20 @@
     return call(keep_kernel, jax.ShapeDtypeStruct(value.shape, value.dtype), [whole()], whole())(value)
 
 
-def combine_kernel(clip_bound, at_ref, squares_ref, *refs):
-    blocks, out_ref = refs[:DP], refs[DP]
+def upright_kernel(*refs):
+    for n in range(DP):
+        refs[DP][n] = refs[n][...].T
+
+
+def combine_kernel(clip_bound, at_ref, squares_ref, blocks_ref, out_ref):
     total = None
     for k in range(DP):
         example = jnp.bitwise_and(at_ref[3] + DP - k, DP - 1)
         squares = jnp.sum(squares_ref[pl.ds(example * X, X)])
         factor = jnp.minimum(1.0, clip_bound * lax.rsqrt(jnp.full((1, LANE), squares, F32) + 1e-06))
-        term = blocks[k][...] * factor
+        term = blocks_ref[k] * factor
         total = term if total is None else total + term
-    out_ref[...] = total.T
+    out_ref[...] = total
 
 
 def turn(n, k):
@@ -217,38 +245,46 @@
     swap = functools.partial(lax.ppermute, axis_name="core", perm=turn(CORE, 1))
     gain = norm_gain.reshape(features // LANE, LANE)
     weight = loss_weight * (1.0 / math.sqrt(doc_length))
-    hidden, gain, weight, at, cto = lax.optimization_barrier((hidden, gain, weight, at, cot.T))
-    ctp = swap(cto)
+    hidden, gain, weight, at = lax.optimization_barrier((hidden, gain, weight, at))
     own, par = [], []
     for half in range(HALVES):
         kept, sent = prep(half, hidden, gain, at)
         own.append(kept)
         par.append(swap(sent))
 
-    def block(k):
-        return product(k, own, par, cto, ctp, at)
-
-    blocks = {k: block(k) for k in (2, 1, 3, 0)}
+    cto = turned(cot)
+    ctp = swap(cto)
+
+    def block(k, chunk):
+        return product(k, chunk, own, par, cto, ctp, at)
+
+    order = [(k, chunk) for chunk in range(2) for k in (2, 1, 3)] + [(0, 0), (0, 1)]
+    blocks = {n: block(*n) for n in order}
     mine, summed = [], []
     for chunk in range(2):
-        arrived = [lax.ppermute(blocks[k][chunk], "x", turn(X, k)) for k in (2, 1, 3)]
-        ready, kept = gather(blocks[0][chunk], *arrived, at)
+        arrived = []
+        for k in (2, 1, 3):
+            arrived.append(lax.ppermute(blocks[k, chunk], "x", turn(X, k)))
+        ready, kept = gather(blocks[0, chunk], *arrived, at)
         mine.append(kept)
         summed.append(exchanged(ready, "z"))
-    *tiles, squares = finish(mine, summed, at, weight)
-    arrived = [tiles[0]] + [lax.ppermute(tiles[k], "dp", turn(DP, k)) for k in range(1, DP)]
-    arrived[0] = keep(arrived[0])
+    before, partial = first(mine[0], summed[0], at, weight)
+    *tiles, squares = last(mine[1], summed[1], before, partial, at, weight)
+    arrived = [lax.ppermute(tiles[k], "dp", turn(DP, k)) for k in range(1, DP)]
+    kept = keep(tiles[0])
     squares = exchanged(squares, ("z", "core"))
     squares = call(pass_kernel, jax.ShapeDtypeStruct((DP * X, 1, LANE), F32), [whole()], whole())(squares)
+    shape = jax.ShapeDtypeStruct((DP, LANE, outs // DP), F32)
+    blocks = call(upright_kernel, shape, [whole()] * DP, whole())(kept, *arrived)
     squares = exchanged(squares, ("dp", "x"))
     clip_bound = math.sqrt(features * outs)
     return call(
         functools.partial(combine_kernel, clip_bound),
         jax.ShapeDtypeStruct((LANE, outs // DP), F32),
-        [whole()] * (DP + 1),
+        [whole()] * 2,
         whole(),
         scalars=1,
-    )(at, squares, *arrived)
+    )(at, squares, blocks)
 
 
 def solution(mesh):

time: 137 us -> 142 us (1.036)
  blocking collectives: 34.9 us -> 14.4 us
  waiting for transfers between devices: 51 us -> 61.8 us
  starting transfers between devices: 26.5 us -> 32.5 us
  Pallas kernels: 17.6 us -> 22.4 us
  local copies, waits for them, and re-layouts: 5.39 us -> 9.71 us
    all_to_all x2 -> x1, blocking collectives: 34.9 us -> 14.4 us  [exchanged(): return lax.all_to_all(value, axis, split_axis=0, concat_axis=0, tiled=True)]
    all_to_all x2 -> x3, waiting for transfers between devices: 6.28 us -> 18.8 us  [exchanged(): return lax.all_to_all(value, axis, split_axis=0, concat_axis=0, tiled=True)]
    all_to_all x2 -> x3, starting transfers between devices: 11.7 us -> 18 us  [exchanged(): return lax.all_to_all(value, axis, split_axis=0, concat_axis=0, tiled=True)]
    pallas_call x5 -> x12, Pallas kernels: 8.07 us -> 12.8 us  [the longest x8 10.1 us: product(): call(functools.partial(product_kernel, turns, chunk), jax.ShapeDtypeStruc...]
    unnamed x5 -> x22, local copies, waits for them, and re-layouts: 5.39 us -> 9.71 us
  transfers between devices with their start and end apart: 14 -> 15, of which waited for: 8 -> 9; matrix products, arithmetic and copies ran while one was open for 0% -> 0% of each run, Pallas kernels for 7% -> 11%
where the time goes in v3:
time: 142 us
  waiting for transfers between devices  61.8 us (44%)
  starting transfers between devices  32.5 us (23%)
  Pallas kernels  22.4 us (16%)
  blocking collectives  14.4 us (10%)
  local copies, waits for them, and re-layouts  9.71 us (7%)
    ppermute x6, waiting for transfers between devices, per_device(): arrived.append(lax.ppermute(blocks[k, chunk], 'x', turn(X, k)))  38.9 us
    all_to_all x3, waiting for transfers between devices, exchanged(): return lax.all_to_all(value, axis, split_axis=0, concat_axis=0, tiled=True)  18.8 us
    all_to_all x3, starting transfers between devices, exchanged(): return lax.all_to_all(value, axis, split_axis=0, concat_axis=0, tiled=True)  18 us
    all_to_all x1, blocking collectives, exchanged(): return lax.all_to_all(value, axis, split_axis=0, concat_axis=0, tiled=True)  14.4 us
    pallas_call x8, Pallas kernels, product(): call(functools.partial(product_kernel, turns, chunk), jax.ShapeDtypeStruc...  10.1 us
    unnamed x22, local copies, waits for them, and re-layouts  9.71 us
    ppermute x6, starting transfers between devices, per_device(): arrived.append(lax.ppermute(blocks[k, chunk], 'x', turn(X, k)))  6.15 us
    pallas_call x2, Pallas kernels, prep(): call(functools.partial(prep_kernel, half), (part, part), [whole(), whole(...  5.11 us
  transfers between devices with their start and end apart: 15, of which 9 were waited for; matrix products, arithmetic and copies ran while one was open for 0% of the time, Pallas kernels for 11%

profile of v3, /device:TPU:1, one launch (start us, length us, event | category | flops | bytes accessed | tf_op | source)
XLA Modules:
  0.0 141.8 jit_solution(18278846920396651726)
XLA Ops:
  0.7 0.1 pad_add_fusion.at_ref
  0.7 3.4 %copy-done.6 = bf16[1,512,8192]{2,1,0:T(8,128)(2,1)S(1)} copy-done((bf16[1,512,8192]{2,1,0:T(8,128)(2,1)S(1)}, bf16[1,512,8192]{2,1,0:T(8,128)(2,1)}, u32[]{:S(2)}) %copy-start.6) | copy-done | bytes 8388632
  4.1 0.8 copy-done.9
  4.9 2.6 %shard_map.47 = (bf16[256,4096]{1,0:T(8,128)(2,1)S(1)}, bf16[256,4096]{1,0:T(8,128)(2,1)S(1)}) custom-call(s32[4]{0:T(128)S(1)} %pad_add_fusion.at_ref, bf16[512,8192]{1,0:T(8,128)(2,1)S(1)} %bitcast.7, f32[64,128]{1,0:T(8,128)S(1)} %bitcast.10), custom_call_target="tpu_custom_call" | custom-call | flops 8388608 | bytes 8388608 | tf_op jit(solution)/shard_map/pallas_call | solution.py:67
  7.4 0.0 copy-start.7
  7.5 3.3 %collective-permute-start.1 = (bf16[256,4096]{1,0:T(8,128)(2,1)S(1)}, bf16[256,4096]{1,0:T(8,128)(2,1)S(1)}, u32[]{:S(2)}, u32[]{:S(2)}) collective-permute-start(bf16[256,4096]{1,0:T(8,128)(2,1)S(1)} %get-tuple-element.31), channel_id=1, source_target_pairs={{0,1},{1,0},{2,3},{3,2},{4,5},{5,4},{6,7},{7,6},{8,9},{9,8},{10,11... | collective-permute-start | bytes 6291464 | tf_op jit(solution)/shard_map/ppermute | solution.py:253
  10.7 0.0 copy-done.10
  10.7 2.6 %shard_map.46 = (bf16[256,4096]{1,0:T(8,128)(2,1)S(1)}, bf16[256,4096]{1,0:T(8,128)(2,1)S(1)}) custom-call(s32[4]{0:T(128)S(1)} %pad_add_fusion.at_ref, bf16[512,8192]{1,0:T(8,128)(2,1)S(1)} %bitcast.8, f32[64,128]{1,0:T(8,128)S(1)} %bitcast.11), custom_call_target="tpu_custom_call" | custom-call | flops 8388608 | bytes 8388608 | tf_op jit(solution)/shard_map/pallas_call | solution.py:67
  13.3 0.0 copy-start.2
  13.3 0.1 collective-permute-start
  13.4 0.0 copy-done.7
  13.4 0.2 shard_map.48.refs_4_
  13.6 0.6 collective-permute-start.2
  14.2 4.1 %collective-permute-done.2.refs_5_ = bf16[512,512]{1,0:T(8,128)(2,1)S(1)} collective-permute-done((bf16[512,512]{1,0:T(8,128)(2,1)S(1)}, bf16[512,512]{1,0:T(8,128)(2,1)S(1)}, u32[]{:S(2)}, u32[]{:S(2)}) %collective-permute-start.2) | collective-permute-done | bytes 524320 | tf_op jit(solution)/shard_map/ppermute | solution.py:256
  18.3 0.0 collective-permute-done.1.refs_3_
  18.3 0.0 collective-permute-done.refs_2_
  18.3 0.0 copy-start.4
  18.3 1.3 shard_map.57
  19.6 0.8 collective-permute-start.8
  20.5 1.3 shard_map.56
  21.7 0.8 collective-permute-start.7
  22.5 1.3 shard_map.55
  23.8 1.1 collective-permute-start.6
  24.9 0.0 copy-done.2
  24.9 0.0 copy-done
  24.9 1.3 shard_map.54.own_ref
  26.2 6.6 %collective-permute-done.8.r3_ref = bf16[2048,128]{1,0:T(8,128)(2,1)S(1)} collective-permute-done((bf16[2048,128]{1,0:T(8,128)(2,1)S(1)}, bf16[2048,128]{1,0:T(8,128)(2,1)S(1)}, u32[]{:S(2)}, u32[]{:S(2)}) %collective-permute-start.8) | collective-permute-done | bytes 524320 | tf_op jit(solution)/shard_map/ppermute | solution.py:267
  32.8 4.0 %collective-permute-done.7.r2_ref = bf16[2048,128]{1,0:T(8,128)(2,1)S(1)} collective-permute-done((bf16[2048,128]{1,0:T(8,128)(2,1)S(1)}, bf16[2048,128]{1,0:T(8,128)(2,1)S(1)}, u32[]{:S(2)}, u32[]{:S(2)}) %collective-permute-start.7) | collective-permute-done | bytes 524320 | tf_op jit(solution)/shard_map/ppermute | solution.py:267
  36.8 9.4 %collective-permute-done.6.r1_ref = bf16[2048,128]{1,0:T(8,128)(2,1)S(1)} collective-permute-done((bf16[2048,128]{1,0:T(8,128)(2,1)S(1)}, bf16[2048,128]{1,0:T(8,128)(2,1)S(1)}, u32[]{:S(2)}, u32[]{:S(2)}) %collective-permute-start.6) | collective-permute-done | bytes 524320 | tf_op jit(solution)/shard_map/ppermute | solution.py:267
  46.2 0.8 shard_map.58
  47.1 0.0 copy-start.8
  47.1 0.8 copy-done.8
  47.9 8.2 %all-to-all-start.1 = ((bf16[8,256,128]{2,1,0:T(8,128)(2,1)}), bf16[8,256,128]{2,1,0:T(8,128)(2,1)}, u32[]{:S(2)}, u32[]{:S(2)}) async-start(bf16[8,256,128]{2,1,0:T(8,128)(2,1)} %copy-done.8), calls=%async_computation.1 | async-start | bytes 1048576 | tf_op jit(solution)/shard_map/all_to_all | solution.py:236
  56.0 1.6 %copy-done.1 = bf16[256,4096]{1,0:T(8,128)(2,1)S(1)} copy-done((bf16[256,4096]{1,0:T(8,128)(2,1)S(1)}, bf16[256,4096]{1,0:T(8,128)(2,1)}, u32[]{:S(2)}) %copy-start.1) | copy-done | bytes 2097176
  57.6 1.6 %copy-done.3 = bf16[256,4096]{1,0:T(8,128)(2,1)S(1)} copy-done((bf16[256,4096]{1,0:T(8,128)(2,1)S(1)}, bf16[256,4096]{1,0:T(8,128)(2,1)}, u32[]{:S(2)}) %copy-start.3) | copy-done | bytes 2097176
  59.2 1.6 %copy-done.5 = bf16[256,4096]{1,0:T(8,128)(2,1)S(1)} copy-done((bf16[256,4096]{1,0:T(8,128)(2,1)S(1)}, bf16[256,4096]{1,0:T(8,128)(2,1)}, u32[]{:S(2)}) %copy-start.5) | copy-done | bytes 2097176
  60.8 1.3 shard_map.52
  62.1 0.3 collective-permute-start.5
  62.3 1.3 shard_map.51
  63.6 1.5 %collective-permute-start.4 = (bf16[2048,128]{1,0:T(8,128)(2,1)S(1)}, bf16[2048,128]{1,0:T(8,128)(2,1)S(1)}, u32[]{:S(2)}, u32[]{:S(2)}) collective-permute-start(bf16[2048,128]{1,0:T(8,128)(2,1)S(1)} %shard_map.51), channel_id=1, source_target_pairs={{0,16},{16,32},{32,48},{48,0},{1,17},{17,33},{33,49},{49,1},{2,18}... | collective-permute-start | bytes 1572872 | tf_op jit(solution)/shard_map/ppermute | solution.py:267
  65.1 1.3 shard_map.50
  66.4 1.6 %collective-permute-start.3 = (bf16[2048,128]{1,0:T(8,128)(2,1)S(1)}, bf16[2048,128]{1,0:T(8,128)(2,1)S(1)}, u32[]{:S(2)}, u32[]{:S(2)}) collective-permute-start(bf16[2048,128]{1,0:T(8,128)(2,1)S(1)} %shard_map.50), channel_id=1, source_target_pairs={{0,32},{16,48},{32,0},{48,16},{1,33},{17,49},{33,1},{49,17},{2,34}... | collective-permute-start | bytes 1572872 | tf_op jit(solution)/shard_map/ppermute | solution.py:267
  68.0 1.3 shard_map.49.own_ref
  69.3 3.9 %collective-permute-done.5.r3_ref = bf16[2048,128]{1,0:T(8,128)(2,1)S(1)} collective-permute-done((bf16[2048,128]{1,0:T(8,128)(2,1)S(1)}, bf16[2048,128]{1,0:T(8,128)(2,1)S(1)}, u32[]{:S(2)}, u32[]{:S(2)}) %collective-permute-start.5) | collective-permute-done | bytes 524320 | tf_op jit(solution)/shard_map/ppermute | solution.py:267
  73.2 2.5 %collective-permute-done.4.r2_ref = bf16[2048,128]{1,0:T(8,128)(2,1)S(1)} collective-permute-done((bf16[2048,128]{1,0:T(8,128)(2,1)S(1)}, bf16[2048,128]{1,0:T(8,128)(2,1)S(1)}, u32[]{:S(2)}, u32[]{:S(2)}) %collective-permute-start.4) | collective-permute-done | bytes 524320 | tf_op jit(solution)/shard_map/ppermute | solution.py:267
  75.7 12.5 %collective-permute-done.3.r1_ref = bf16[2048,128]{1,0:T(8,128)(2,1)S(1)} collective-permute-done((bf16[2048,128]{1,0:T(8,128)(2,1)S(1)}, bf16[2048,128]{1,0:T(8,128)(2,1)S(1)}, u32[]{:S(2)}, u32[]{:S(2)}) %collective-permute-start.3) | collective-permute-done | bytes 524320 | tf_op jit(solution)/shard_map/ppermute | solution.py:267
  88.2 1.6 %shard_map.53 = (bf16[8,256,128]{2,1,0:T(8,128)(2,1)}, f32[256,128]{1,0:T(8,128)S(1)}) custom-call(s32[4]{0:T(128)S(1)} %pad_add_fusion.at_ref, f32[2048,128]{1,0:T(8,128)S(1)} %shard_map.49.own_ref, bf16[2048,128]{1,0:T(8,128)(2,1)S(1)} %collective-permute-done.3.r1_ref, bf16[2048,128]{1,0:T(8,128)(2,1)S(1)} %collective-permute-done.4.r2_ref, ...), custom_call_target="tpu_custom_call" | custom-call | flops 1048576 | bytes 3145728 | tf_op jit(solution)/shard_map/pallas_call | solution.py:138
  89.8 0.0 all-to-all-done.1.arrived_ref
  89.8 6.4 %all-to-all-start = ((bf16[8,256,128]{2,1,0:T(8,128)(2,1)}), bf16[8,256,128]{2,1,0:T(8,128)(2,1)S(1)}, u32[]{:S(2)}, u32[]{:S(2)}) async-start(bf16[8,256,128]{2,1,0:T(8,128)(2,1)} %get-tuple-element.33), calls=%async_computation | async-start | bytes 1048576 | tf_op jit(solution)/shard_map/all_to_all | solution.py:236
  96.2 1.7 %shard_map.59 = (f32[256,128]{1,0:T(8,128)S(1)}, f32[8,128]{1,0:T(8,128)S(1)}) custom-call(s32[4]{0:T(128)S(1)} %pad_add_fusion.at_ref, f32[1]{0:T(128)S(6)} %mul.3.weight_ref, f32[256,128]{1,0:T(8,128)S(1)} %get-tuple-element.34.mine_ref, bf16[8,256,128]{2,1,0:T(8,128)(2,1)} %all-to-all-done.1.arrived_ref), custom_call_target="tpu_custom_call" | custom-call | flops 1048576 | bytes 1048576 | tf_op jit(solution)/shard_map/pallas_call | solution.py:164
  97.9 12.7 %all-to-all-done.arrived_ref = bf16[8,256,128]{2,1,0:T(8,128)(2,1)S(1)} async-done(((bf16[8,256,128]{2,1,0:T(8,128)(2,1)}), bf16[8,256,128]{2,1,0:T(8,128)(2,1)S(1)}, u32[]{:S(2)}, u32[]{:S(2)}) %all-to-all-start) | async-done | bytes 524320 | tf_op jit(solution)/shard_map/all_to_all | solution.py:236
  110.5 0.7 shard_map.60
  111.2 2.9 %collective-permute-start.10 = (f32[128,128]{1,0:T(8,128)S(1)}, f32[128,128]{1,0:T(8,128)S(1)}, u32[]{:S(2)}, u32[]{:S(2)}) collective-permute-start(f32[128,128]{1,0:T(8,128)S(1)} %get-tuple-element.41), channel_id=1, source_target_pairs={{0,128},{64,192},{128,0},{192,64},{1,129},{65,193},{129,1},{193,65... | collective-permute-start | bytes 196616 | tf_op jit(solution)/shard_map/ppermute | solution.py:273
  114.2 0.8 collective-permute-start.11
  114.9 0.7 collective-permute-start.9
  115.6 14.4 %all_to_all.20.in_ref = f32[16,1,128]{2,1,0:T(1,128)S(1)} all-to-all(f32[16,1,128]{2,1,0:T(1,128)S(1)} %get-tuple-element.38), channel_id=1, replica_groups=mesh['dp'=4,'x'=4,'z'=8,'core'=2] {'z','core'}, dimensions={0} | all-to-all | bytes 16384 | tf_op jit(solution)/shard_map/all_to_all | solution.py:236
  130.0 0.6 shard_map.61
  130.7 3.5 %all-to-all-start.3 = ((f32[16,1,128]{2,1,0:T(1,128)}), f32[16,1,128]{2,1,0:T(1,128)S(1)}, u32[]{:S(2)}, u32[]{:S(2)}) async-start(f32[16,1,128]{2,1,0:T(1,128)} %shard_map.61), calls=%async_computation.3 | async-start | bytes 16384 | tf_op jit(solution)/shard_map/all_to_all | solution.py:236
  134.2 0.0 collective-permute-done.10.refs_2_
  134.2 0.0 collective-permute-done.11.refs_3_
  134.2 0.0 collective-permute-done.9.refs_1_
  134.2 0.1 shard_map.63.blocks_ref
  134.3 6.1 %all-to-all-done.3.squares_ref = f32[16,1,128]{2,1,0:T(1,128)S(1)} async-done(((f32[16,1,128]{2,1,0:T(1,128)}), f32[16,1,128]{2,1,0:T(1,128)S(1)}, u32[]{:S(2)}, u32[]{:S(2)}) %all-to-all-start.3) | async-done | bytes 8224 | tf_op jit(solution)/shard_map/all_to_all | solution.py:236
  140.4 1.3 shard_map.64
  (9 shorter events, 0.0 us)
Async XLA Ops:
  0.7 3.4 %copy-start.6 = (bf16[1,512,8192]{2,1,0:T(8,128)(2,1)S(1)}, bf16[1,512,8192]{2,1,0:T(8,128)(2,1)}, u32[]{:S(2)}) copy-start(bf16[1,512,8192]{2,1,0:T(8,128)(2,1)} %param.4) | copy-start | bytes 25165828
  4.1 0.8 copy-start.9
  4.9 5.9 %copy-start.10 = (f32[8192]{0:T(1024)S(1)}, f32[8192]{0:T(1024)}, u32[]{:S(2)}) copy-start(f32[8192]{0:T(1024)} %param.5) | copy-start | bytes 98308
  7.4 6.0 %copy-start.7 = (bf16[1,512,512]{2,1,0:T(8,128)(2,1)S(1)}, bf16[1,512,512]{2,1,0:T(8,128)(2,1)}, u32[]{:S(2)}) copy-start(bf16[1,512,512]{2,1,0:T(8,128)(2,1)} %param.6) | copy-start | bytes 1572868
  7.5 10.9 %collective-permute-start.1 = (bf16[256,4096]{1,0:T(8,128)(2,1)S(1)}, bf16[256,4096]{1,0:T(8,128)(2,1)S(1)}, u32[]{:S(2)}, u32[]{:S(2)}) collective-permute-start(bf16[256,4096]{1,0:T(8,128)(2,1)S(1)} %get-tuple-element.31), channel_id=1, source_target_pairs={{0,1},{1,0},{2,3},{3,2},{4,5},{5,4},{6,7},{7,6},{8,9},{9,8},{10,11... | collective-permute-start | bytes 6291464 | tf_op jit(solution)/shard_map/ppermute | solution.py:253
  13.3 11.6 %copy-start.2 = (bf16[256,4096]{1,0:T(8,128)(2,1)}, bf16[256,4096]{1,0:T(8,128)(2,1)S(1)}, u32[]{:S(2)}) copy-start(bf16[256,4096]{1,0:T(8,128)(2,1)S(1)} %get-tuple-element.28.refs_0_) | copy-start | bytes 6291460
  13.3 5.0 %collective-permute-start = (bf16[256,4096]{1,0:T(8,128)(2,1)S(1)}, bf16[256,4096]{1,0:T(8,128)(2,1)S(1)}, u32[]{:S(2)}, u32[]{:S(2)}) collective-permute-start(bf16[256,4096]{1,0:T(8,128)(2,1)S(1)} %get-tuple-element.30), channel_id=1, source_target_pairs={{0,1},{1,0},{2,3},{3,2},{4,5},{5,4},{6,7},{7,6},{8,9},{9,8},{10,11... | collective-permute-start | bytes 6291464 | tf_op jit(solution)/shard_map/ppermute | solution.py:253
  13.6 4.7 %collective-permute-start.2 = (bf16[512,512]{1,0:T(8,128)(2,1)S(1)}, bf16[512,512]{1,0:T(8,128)(2,1)S(1)}, u32[]{:S(2)}, u32[]{:S(2)}) collective-permute-start(bf16[512,512]{1,0:T(8,128)(2,1)S(1)} %shard_map.48.refs_4_), channel_id=1, source_target_pairs={{0,1},{1,0},{2,3},{3,2},{4,5},{5,4},{6,7},{7,6},{8,9},{9,8},{10,11... | collective-permute-start | bytes 1572872 | tf_op jit(solution)/shard_map/ppermute | solution.py:256
  18.3 6.6 %copy-start = (bf16[256,4096]{1,0:T(8,128)(2,1)}, bf16[256,4096]{1,0:T(8,128)(2,1)S(1)}, u32[]{:S(2)}) copy-start(bf16[256,4096]{1,0:T(8,128)(2,1)S(1)} %collective-permute-done.1.refs_3_) | copy-start | bytes 6291460
  18.3 6.6 %copy-start.4 = (bf16[256,4096]{1,0:T(8,128)(2,1)}, bf16[256,4096]{1,0:T(8,128)(2,1)S(1)}, u32[]{:S(2)}) copy-start(bf16[256,4096]{1,0:T(8,128)(2,1)S(1)} %collective-permute-done.refs_2_) | copy-start | bytes 6291460
  19.6 13.2 %collective-permute-start.8 = (bf16[2048,128]{1,0:T(8,128)(2,1)S(1)}, bf16[2048,128]{1,0:T(8,128)(2,1)S(1)}, u32[]{:S(2)}, u32[]{:S(2)}) collective-permute-start(bf16[2048,128]{1,0:T(8,128)(2,1)S(1)} %shard_map.57), channel_id=1, source_target_pairs={{0,48},{16,0},{32,16},{48,32},{1,49},{17,1},{33,17},{49,33},{2,50}... | collective-permute-start | bytes 1572872 | tf_op jit(solution)/shard_map/ppermute | solution.py:267
  21.7 15.1 %collective-permute-start.7 = (bf16[2048,128]{1,0:T(8,128)(2,1)S(1)}, bf16[2048,128]{1,0:T(8,128)(2,1)S(1)}, u32[]{:S(2)}, u32[]{:S(2)}) collective-permute-start(bf16[2048,128]{1,0:T(8,128)(2,1)S(1)} %shard_map.56), channel_id=1, source_target_pairs={{0,16},{16,32},{32,48},{48,0},{1,17},{17,33},{33,49},{49,1},{2,18}... | collective-permute-start | bytes 1572872 | tf_op jit(solution)/shard_map/ppermute | solution.py:267
  23.8 22.5 %collective-permute-start.6 = (bf16[2048,128]{1,0:T(8,128)(2,1)S(1)}, bf16[2048,128]{1,0:T(8,128)(2,1)S(1)}, u32[]{:S(2)}, u32[]{:S(2)}) collective-permute-start(bf16[2048,128]{1,0:T(8,128)(2,1)S(1)} %shard_map.55), channel_id=1, source_target_pairs={{0,32},{16,48},{32,0},{48,16},{1,33},{17,49},{33,1},{49,17},{2,34}... | collective-permute-start | bytes 1572872 | tf_op jit(solution)/shard_map/ppermute | solution.py:267
  47.1 0.8 copy-start.8
  47.9 41.9 %all-to-all-start.1 = ((bf16[8,256,128]{2,1,0:T(8,128)(2,1)}), bf16[8,256,128]{2,1,0:T(8,128)(2,1)}, u32[]{:S(2)}, u32[]{:S(2)}) async-start(bf16[8,256,128]{2,1,0:T(8,128)(2,1)} %copy-done.8), calls=%async_computation.1 | async-start | bytes 1048576 | tf_op jit(solution)/shard_map/all_to_all | solution.py:236
  56.0 1.6 %copy-start.1 = (bf16[256,4096]{1,0:T(8,128)(2,1)S(1)}, bf16[256,4096]{1,0:T(8,128)(2,1)}, u32[]{:S(2)}) copy-start(bf16[256,4096]{1,0:T(8,128)(2,1)} %copy-done) | copy-start | bytes 6291460
  57.6 1.6 %copy-start.3 = (bf16[256,4096]{1,0:T(8,128)(2,1)S(1)}, bf16[256,4096]{1,0:T(8,128)(2,1)}, u32[]{:S(2)}) copy-start(bf16[256,4096]{1,0:T(8,128)(2,1)} %copy-done.2) | copy-start | bytes 6291460
  59.2 1.6 %copy-start.5 = (bf16[256,4096]{1,0:T(8,128)(2,1)S(1)}, bf16[256,4096]{1,0:T(8,128)(2,1)}, u32[]{:S(2)}) copy-start(bf16[256,4096]{1,0:T(8,128)(2,1)} %copy-done.4) | copy-start | bytes 6291460
  62.1 11.2 %collective-permute-start.5 = (bf16[2048,128]{1,0:T(8,128)(2,1)S(1)}, bf16[2048,128]{1,0:T(8,128)(2,1)S(1)}, u32[]{:S(2)}, u32[]{:S(2)}) collective-permute-start(bf16[2048,128]{1,0:T(8,128)(2,1)S(1)} %shard_map.52), channel_id=1, source_target_pairs={{0,48},{16,0},{32,16},{48,32},{1,49},{17,1},{33,17},{49,33},{2,50}... | collective-permute-start | bytes 1572872 | tf_op jit(solution)/shard_map/ppermute | solution.py:267
  63.6 12.1 %collective-permute-start.4 = (bf16[2048,128]{1,0:T(8,128)(2,1)S(1)}, bf16[2048,128]{1,0:T(8,128)(2,1)S(1)}, u32[]{:S(2)}, u32[]{:S(2)}) collective-permute-start(bf16[2048,128]{1,0:T(8,128)(2,1)S(1)} %shard_map.51), channel_id=1, source_target_pairs={{0,16},{16,32},{32,48},{48,0},{1,17},{17,33},{33,49},{49,1},{2,18}... | collective-permute-start | bytes 1572872 | tf_op jit(solution)/shard_map/ppermute | solution.py:267
  66.4 21.8 %collective-permute-start.3 = (bf16[2048,128]{1,0:T(8,128)(2,1)S(1)}, bf16[2048,128]{1,0:T(8,128)(2,1)S(1)}, u32[]{:S(2)}, u32[]{:S(2)}) collective-permute-start(bf16[2048,128]{1,0:T(8,128)(2,1)S(1)} %shard_map.50), channel_id=1, source_target_pairs={{0,32},{16,48},{32,0},{48,16},{1,33},{17,49},{33,1},{49,17},{2,34}... | collective-permute-start | bytes 1572872 | tf_op jit(solution)/shard_map/ppermute | solution.py:267
  89.8 20.7 %all-to-all-start = ((bf16[8,256,128]{2,1,0:T(8,128)(2,1)}), bf16[8,256,128]{2,1,0:T(8,128)(2,1)S(1)}, u32[]{:S(2)}, u32[]{:S(2)}) async-start(bf16[8,256,128]{2,1,0:T(8,128)(2,1)} %get-tuple-element.33), calls=%async_computation | async-start | bytes 1048576 | tf_op jit(solution)/shard_map/all_to_all | solution.py:236
  111.2 22.9 %collective-permute-start.10 = (f32[128,128]{1,0:T(8,128)S(1)}, f32[128,128]{1,0:T(8,128)S(1)}, u32[]{:S(2)}, u32[]{:S(2)}) collective-permute-start(f32[128,128]{1,0:T(8,128)S(1)} %get-tuple-element.41), channel_id=1, source_target_pairs={{0,128},{64,192},{128,0},{192,64},{1,129},{65,193},{129,1},{193,65... | collective-permute-start | bytes 196616 | tf_op jit(solution)/shard_map/ppermute | solution.py:273
  114.2 20.0 %collective-permute-start.11 = (f32[128,128]{1,0:T(8,128)S(1)}, f32[128,128]{1,0:T(8,128)S(1)}, u32[]{:S(2)}, u32[]{:S(2)}) collective-permute-start(f32[128,128]{1,0:T(8,128)S(1)} %get-tuple-element.42), channel_id=1, source_target_pairs={{0,192},{64,0},{128,64},{192,128},{1,193},{65,1},{129,65},{193,129... | collective-permute-start | bytes 196616 | tf_op jit(solution)/shard_map/ppermute | solution.py:273
  114.9 19.2 %collective-permute-start.9 = (f32[128,128]{1,0:T(8,128)S(1)}, f32[128,128]{1,0:T(8,128)S(1)}, u32[]{:S(2)}, u32[]{:S(2)}) collective-permute-start(f32[128,128]{1,0:T(8,128)S(1)} %get-tuple-element.40), channel_id=1, source_target_pairs={{0,64},{64,128},{128,192},{192,0},{1,65},{65,129},{129,193},{193,1... | collective-permute-start | bytes 196616 | tf_op jit(solution)/shard_map/ppermute | solution.py:273
  130.7 9.8 %all-to-all-start.3 = ((f32[16,1,128]{2,1,0:T(1,128)}), f32[16,1,128]{2,1,0:T(1,128)S(1)}, u32[]{:S(2)}, u32[]{:S(2)}) async-start(f32[16,1,128]{2,1,0:T(1,128)} %shard_map.61), calls=%async_computation.3 | async-start | bytes 16384 | tf_op jit(solution)/shard_map/all_to_all | solution.py:236

commit v4 on v3

--- a/solution.py
+++ b/solution.py
@@ -17,6 +17,8 @@
 F32 = jnp.float32
 HALVES = 2
 PIECES = 4
+CUTS = (0, 192, 384, 512)
+CHUNKS = range(len(CUTS) - 1)
 
 
 def call(kernel, out_shape, in_specs, out_specs, scalars=0, scratch=(), flops=0, moved=0, mib=12):
@@ -89,14 +91,15 @@
     tokens = refs[: 2 * HALVES]
     cot_refs = refs[2 * HALVES : 2 * HALVES + 2]
     out_ref = refs[2 * HALVES + 2]
-    half = cot_refs[0].shape[0] // 2
+    cut = slice(CUTS[chunk], CUTS[chunk + 1])
+    half = CUTS[chunk + 1] - CUTS[chunk]
     rows = tokens[0].shape[0]
     for p in range(Z // 2):
         lanes = pl.ds(pl.multiple_of(owner * (Z * LANE) + p * 2 * LANE, 2 * LANE), 2 * LANE)
         total = None
         for n, t in enumerate(tokens):
             c = cot_refs[n // HALVES]
-            c = c[chunk * half : (chunk + 1) * half, (n % HALVES) * rows : (n % HALVES + 1) * rows]
+            c = c[cut, (n % HALVES) * rows : (n % HALVES + 1) * rows]
             term = jnp.dot(c, t[:, lanes], preferred_element_type=F32)
             total = term if total is None else total + term
         for i in range(2):
@@ -105,7 +108,7 @@
 
 
 def product(turns, chunk, own, par, cto, ctp, at):
-    outs = cto.shape[0] // 2
+    outs = CUTS[chunk + 1] - CUTS[chunk]
     tokens = 2 * cto.shape[1]
     return call(
         functools.partial(product_kernel, turns, chunk),
@@ -172,32 +175,33 @@
     )(at, weight, mine, arrived)
 
 
-def last_kernel(at_ref, weight_ref, mine_ref, arrived_ref, before_ref, partial_ref, *refs):
-    outs, squares_ref, tile = refs[:DP], refs[DP], refs[DP + 1]
+def last_kernel(at_ref, weight_ref, mine_ref, arrived_ref, *refs):
+    before = refs[: 2 * len(CHUNKS) - 2]
+    outs, squares_ref, tile = refs[len(before) : len(before) + DP], refs[-2], refs[-1]
     total, squares = finished(at_ref, weight_ref, mine_ref, arrived_ref)
-    half = total.shape[0]
-    squares_ref[...] = jnp.broadcast_to((squares + partial_ref[:1, :])[None], squares_ref.shape)
-    tile[:half, :] = before_ref[...]
-    tile[half:, :] = total
-    rows = 2 * half // DP
+    for n in CHUNKS[:-1]:
+        tile[CUTS[n] : CUTS[n + 1], :] = before[2 * n][...]
+        squares = squares + before[2 * n + 1][:1, :]
+    squares_ref[...] = jnp.broadcast_to(squares[None], squares_ref.shape)
+    tile[CUTS[-2] :, :] = total
+    rows = CUTS[-1] // DP
     for k in range(DP):
         owner = jnp.bitwise_and(at_ref[3] + k, DP - 1)
         outs[k][...] = tile[pl.ds(pl.multiple_of(owner * rows, rows), rows), :]
 
 
-def last(mine, arrived, before, partial, at, weight):
-    half = mine.shape[0]
-    block = jax.ShapeDtypeStruct((2 * half // DP, LANE), F32)
+def last(mine, arrived, before, at, weight):
+    block = jax.ShapeDtypeStruct((CUTS[-1] // DP, LANE), F32)
     return call(
         last_kernel,
         (block,) * DP + (jax.ShapeDtypeStruct((Z * CORE, 1, LANE), F32),),
-        [pl.BlockSpec(memory_space=pltpu.SMEM)] + [whole()] * 4,
+        [pl.BlockSpec(memory_space=pltpu.SMEM)] + [whole()] * (2 + len(before)),
         (whole(),) * (DP + 1),
         scalars=1,
-        scratch=[VMEM((2 * half, LANE), F32)],
+        scratch=[VMEM((CUTS[-1], LANE), F32)],
         flops=4 * arrived.size,
         moved=4 * arrived.size,
-    )(at, weight, mine, arrived, before, partial)
+    )(at, weight, mine, arrived, *before)
 
 
 def pass_kernel(in_ref, out_ref):
@@ -221,8 +225,8 @@
     total = None
     for k in range(DP):
         example = jnp.bitwise_and(at_ref[3] + DP - k, DP - 1)
-        squares = jnp.sum(squares_ref[pl.ds(example * X, X)])
-        factor = jnp.minimum(1.0, clip_bound * lax.rsqrt(jnp.full((1, LANE), squares, F32) + 1e-06))
+        squares = jnp.sum(jnp.sum(squares_ref[pl.ds(example * X, X)], axis=0), axis=1, keepdims=True)
+        factor = jnp.minimum(1.0, clip_bound * lax.rsqrt(squares + 1e-06))
         term = blocks_ref[k] * factor
         total = term if total is None else total + term
     out_ref[...] = total
@@ -258,18 +262,20 @@
     def block(k, chunk):
         return product(k, chunk, own, par, cto, ctp, at)
 
-    order = [(k, chunk) for chunk in range(2) for k in (2, 1, 3)] + [(0, 0), (0, 1)]
+    order = [(k, chunk) for chunk in CHUNKS for k in (2, 1, 3)] + [(0, chunk) for chunk in CHUNKS]
     blocks = {n: block(*n) for n in order}
     mine, summed = [], []
-    for chunk in range(2):
+    for chunk in CHUNKS:
         arrived = []
         for k in (2, 1, 3):
             arrived.append(lax.ppermute(blocks[k, chunk], "x", turn(X, k)))
         ready, kept = gather(blocks[0, chunk], *arrived, at)
         mine.append(kept)
         summed.append(exchanged(ready, "z"))
-    before, partial = first(mine[0], summed[0], at, weight)
-    *tiles, squares = last(mine[1], summed[1], before, partial, at, weight)
+    before = []
+    for n in CHUNKS[:-1]:
+        before += first(mine[n], summed[n], at, weight)
+    *tiles, squares = last(mine[-1], summed[-1], before, at, weight)
     arrived = [lax.ppermute(tiles[k], "dp", turn(DP, k)) for k in range(1, DP)]
     kept = keep(tiles[0])
     squares = exchanged(squares, ("z", "core"))

time: 142 us -> 155 us (1.092)
  waiting for transfers between devices: 61.8 us -> 51.5 us
  starting transfers between devices: 32.5 us -> 41.5 us
  local copies, waits for them, and re-layouts: 9.71 us -> 17.4 us
  Pallas kernels: 22.4 us -> 26.3 us
  blocking collectives: 14.4 us -> 16.8 us
    unnamed x22 -> x36, local copies, waits for them, and re-layouts: 9.71 us -> 17.4 us
    all_to_all x3 -> x4, waiting for transfers between devices: 18.8 us -> 12.3 us  [exchanged(): return lax.all_to_all(value, axis, split_axis=0, concat_axis=0, tiled=True)]
    all_to_all x3 -> x4, starting transfers between devices: 18 us -> 24.4 us  [exchanged(): return lax.all_to_all(value, axis, split_axis=0, concat_axis=0, tiled=True)]
    ppermute x6 -> x9, waiting for transfers between devices: 38.9 us -> 35.1 us  [per_device(): arrived.append(lax.ppermute(blocks[k, chunk], 'x', turn(X, k)))]
    pallas_call x8 -> x12, Pallas kernels: 10.1 us -> 13.2 us  [product(): call(functools.partial(product_kernel, turns, chunk), jax.ShapeDtypeStruc...]
    all_to_all x1, blocking collectives: 14.4 us -> 16.8 us  [exchanged(): return lax.all_to_all(value, axis, split_axis=0, concat_axis=0, tiled=True)]
    ppermute x6 -> x9, starting transfers between devices: 6.15 us -> 8.1 us  [per_device(): arrived.append(lax.ppermute(blocks[k, chunk], 'x', turn(X, k)))]
  transfers between devices with their start and end apart: 15 -> 19, of which waited for: 9 -> 12; matrix products, arithmetic and copies ran while one was open for 0% -> 0% of each run, Pallas kernels for 11% -> 13%
where the time goes in v4:
time: 155 us
  waiting for transfers between devices  51.5 us (33%)
  starting transfers between devices  41.5 us (27%)
  Pallas kernels  26.3 us (17%)
  local copies, waits for them, and re-layouts  17.4 us (11%)
  blocking collectives  16.8 us (11%)
    ppermute x9, waiting for transfers between devices, per_device(): arrived.append(lax.ppermute(blocks[k, chunk], 'x', turn(X, k)))  35.1 us
    all_to_all x4, starting transfers between devices, exchanged(): return lax.all_to_all(value, axis, split_axis=0, concat_axis=0, tiled=True)  24.4 us
    unnamed x36, local copies, waits for them, and re-layouts  17.4 us
    all_to_all x1, blocking collectives, exchanged(): return lax.all_to_all(value, axis, split_axis=0, concat_axis=0, tiled=True)  16.8 us
    pallas_call x12, Pallas kernels, product(): call(functools.partial(product_kernel, turns, chunk), jax.ShapeDtypeStruc...  13.2 us
    all_to_all x4, waiting for transfers between devices, exchanged(): return lax.all_to_all(value, axis, split_axis=0, concat_axis=0, tiled=True)  12.3 us
    ppermute x9, starting transfers between devices, per_device(): arrived.append(lax.ppermute(blocks[k, chunk], 'x', turn(X, k)))  8.1 us
    pallas_call x2, Pallas kernels, prep(): call(functools.partial(prep_kernel, half), (part, part), [whole(), whole(...  5.11 us
  transfers between devices with their start and end apart: 19, of which 12 were waited for; matrix products, arithmetic and copies ran while one was open for 0% of the time, Pallas kernels for 13%

profile of v4, /device:TPU:1, one launch (start us, length us, event | category | flops | bytes accessed | tf_op | source)
XLA Modules:
  0.0 154.5 jit_solution(16864552016609715189)
XLA Ops:
  0.7 3.4 %copy-done.9 = bf16[1,512,8192]{2,1,0:T(8,128)(2,1)S(1)} copy-done((bf16[1,512,8192]{2,1,0:T(8,128)(2,1)S(1)}, bf16[1,512,8192]{2,1,0:T(8,128)(2,1)}, u32[]{:S(2)}) %copy-start.9) | copy-done | bytes 8388632
  4.1 0.8 copy-done.13
  4.9 2.6 %shard_map.47 = (bf16[256,4096]{1,0:T(8,128)(2,1)S(1)}, bf16[256,4096]{1,0:T(8,128)(2,1)S(1)}) custom-call(s32[4]{0:T(128)S(1)} %pad_add_fusion.at_ref, bf16[512,8192]{1,0:T(8,128)(2,1)S(1)} %bitcast.7, f32[64,128]{1,0:T(8,128)S(1)} %bitcast.10), custom_call_target="tpu_custom_call" | custom-call | flops 8388608 | bytes 8388608 | tf_op jit(solution)/shard_map/pallas_call | solution.py:69
  7.5 3.3 %collective-permute-start.1 = (bf16[256,4096]{1,0:T(8,128)(2,1)S(1)}, bf16[256,4096]{1,0:T(8,128)(2,1)S(1)}, u32[]{:S(2)}, u32[]{:S(2)}) collective-permute-start(bf16[256,4096]{1,0:T(8,128)(2,1)S(1)} %get-tuple-element.35), channel_id=1, source_target_pairs={{0,1},{1,0},{2,3},{3,2},{4,5},{5,4},{6,7},{7,6},{8,9},{9,8},{10,11... | collective-permute-start | bytes 6291464 | tf_op jit(solution)/shard_map/ppermute | solution.py:257
  10.7 2.6 %shard_map.46 = (bf16[256,4096]{1,0:T(8,128)(2,1)S(1)}, bf16[256,4096]{1,0:T(8,128)(2,1)S(1)}) custom-call(s32[4]{0:T(128)S(1)} %pad_add_fusion.at_ref, bf16[512,8192]{1,0:T(8,128)(2,1)S(1)} %bitcast.8, f32[64,128]{1,0:T(8,128)S(1)} %bitcast.11), custom_call_target="tpu_custom_call" | custom-call | flops 8388608 | bytes 8388608 | tf_op jit(solution)/shard_map/pallas_call | solution.py:69
  13.6 0.6 collective-permute-start.2
  14.2 4.1 %collective-permute-done.2.refs_5_ = bf16[512,512]{1,0:T(8,128)(2,1)S(1)} collective-permute-done((bf16[512,512]{1,0:T(8,128)(2,1)S(1)}, bf16[512,512]{1,0:T(8,128)(2,1)S(1)}, u32[]{:S(2)}, u32[]{:S(2)}) %collective-permute-start.2) | collective-permute-done | bytes 524320 | tf_op jit(solution)/shard_map/ppermute | solution.py:260
  18.3 1.1 shard_map.63
  19.5 0.8 collective-permute-start.11
  20.3 1.1 shard_map.62
  21.5 0.8 collective-permute-start.10
  22.2 1.1 shard_map.61
  23.4 1.1 collective-permute-start.9
  24.5 1.1 shard_map.60.own_ref
  25.7 4.2 %collective-permute-done.11.r3_ref = bf16[1536,128]{1,0:T(8,128)(2,1)S(1)} collective-permute-done((bf16[1536,128]{1,0:T(8,128)(2,1)S(1)}, bf16[1536,128]{1,0:T(8,128)(2,1)S(1)}, u32[]{:S(2)}, u32[]{:S(2)}) %collective-permute-start.11) | collective-permute-done | bytes 393248 | tf_op jit(solution)/shard_map/ppermute | solution.py:271
  29.9 3.9 %collective-permute-done.10.r2_ref = bf16[1536,128]{1,0:T(8,128)(2,1)S(1)} collective-permute-done((bf16[1536,128]{1,0:T(8,128)(2,1)S(1)}, bf16[1536,128]{1,0:T(8,128)(2,1)S(1)}, u32[]{:S(2)}, u32[]{:S(2)}) %collective-permute-start.10) | collective-permute-done | bytes 393248 | tf_op jit(solution)/shard_map/ppermute | solution.py:271
  33.7 6.6 %collective-permute-done.9.r1_ref = bf16[1536,128]{1,0:T(8,128)(2,1)S(1)} collective-permute-done((bf16[1536,128]{1,0:T(8,128)(2,1)S(1)}, bf16[1536,128]{1,0:T(8,128)(2,1)S(1)}, u32[]{:S(2)}, u32[]{:S(2)}) %collective-permute-start.9) | collective-permute-done | bytes 393248 | tf_op jit(solution)/shard_map/ppermute | solution.py:271
  40.3 0.8 shard_map.64
  41.1 0.8 copy-done.12
  41.9 0.6 copy-done.14
  42.5 8.2 %all-to-all-start.2 = ((bf16[8,192,128]{2,1,0:T(8,128)(2,1)}), bf16[8,192,128]{2,1,0:T(8,128)(2,1)S(1)}, u32[]{:S(2)}, u32[]{:S(2)}) async-start(bf16[8,192,128]{2,1,0:T(8,128)(2,1)} %copy-done.12), calls=%async_computation.2 | async-start | bytes 786432 | tf_op jit(solution)/shard_map/all_to_all | solution.py:240
  50.7 1.6 %copy-done.1 = bf16[256,4096]{1,0:T(8,128)(2,1)S(1)} copy-done((bf16[256,4096]{1,0:T(8,128)(2,1)S(1)}, bf16[256,4096]{1,0:T(8,128)(2,1)}, u32[]{:S(2)}) %copy-start.1) | copy-done | bytes 2097176
  52.3 1.6 %copy-done.4 = bf16[256,4096]{1,0:T(8,128)(2,1)S(1)} copy-done((bf16[256,4096]{1,0:T(8,128)(2,1)S(1)}, bf16[256,4096]{1,0:T(8,128)(2,1)}, u32[]{:S(2)}) %copy-start.4) | copy-done | bytes 2097176
  53.9 1.6 %copy-done.7 = bf16[256,4096]{1,0:T(8,128)(2,1)S(1)} copy-done((bf16[256,4096]{1,0:T(8,128)(2,1)S(1)}, bf16[256,4096]{1,0:T(8,128)(2,1)}, u32[]{:S(2)}) %copy-start.7) | copy-done | bytes 2097176
  55.5 1.1 shard_map.57
  56.9 1.1 shard_map.56
  58.0 1.5 collective-permute-start.7
  59.6 1.1 shard_map.55
  60.7 1.6 %collective-permute-start.6 = (bf16[1536,128]{1,0:T(8,128)(2,1)S(1)}, bf16[1536,128]{1,0:T(8,128)(2,1)S(1)}, u32[]{:S(2)}, u32[]{:S(2)}) collective-permute-start(bf16[1536,128]{1,0:T(8,128)(2,1)S(1)} %shard_map.55), channel_id=1, source_target_pairs={{0,32},{16,48},{32,0},{48,16},{1,33},{17,49},{33,1},{49,17},{2,34}... | collective-permute-start | bytes 1179656 | tf_op jit(solution)/shard_map/ppermute | solution.py:271
  62.3 1.1 shard_map.54.own_ref
  63.4 1.5 collective-permute-done.8.r3_ref
  64.9 2.4 %collective-permute-done.7.r2_ref = bf16[1536,128]{1,0:T(8,128)(2,1)S(1)} collective-permute-done((bf16[1536,128]{1,0:T(8,128)(2,1)S(1)}, bf16[1536,128]{1,0:T(8,128)(2,1)S(1)}, u32[]{:S(2)}, u32[]{:S(2)}) %collective-permute-start.7) | collective-permute-done | bytes 393248 | tf_op jit(solution)/shard_map/ppermute | solution.py:271
  67.3 9.6 %collective-permute-done.6.r1_ref = bf16[1536,128]{1,0:T(8,128)(2,1)S(1)} collective-permute-done((bf16[1536,128]{1,0:T(8,128)(2,1)S(1)}, bf16[1536,128]{1,0:T(8,128)(2,1)S(1)}, u32[]{:S(2)}, u32[]{:S(2)}) %collective-permute-start.6) | collective-permute-done | bytes 393248 | tf_op jit(solution)/shard_map/ppermute | solution.py:271
  76.9 0.8 shard_map.58
  77.7 0.7 copy-done.11
  78.4 0.6 copy-done.16
  79.1 6.4 %all-to-all-start.1 = ((bf16[8,192,128]{2,1,0:T(8,128)(2,1)}), bf16[8,192,128]{2,1,0:T(8,128)(2,1)}, u32[]{:S(2)}, u32[]{:S(2)}) async-start(bf16[8,192,128]{2,1,0:T(8,128)(2,1)} %copy-done.11), calls=%async_computation.1 | async-start | bytes 786432 | tf_op jit(solution)/shard_map/all_to_all | solution.py:240
  85.5 1.6 %copy-done.2 = bf16[256,4096]{1,0:T(8,128)(2,1)S(1)} copy-done((bf16[256,4096]{1,0:T(8,128)(2,1)S(1)}, bf16[256,4096]{1,0:T(8,128)(2,1)}, u32[]{:S(2)}) %copy-start.2) | copy-done | bytes 2097176
  87.0 1.6 %copy-done.5 = bf16[256,4096]{1,0:T(8,128)(2,1)S(1)} copy-done((bf16[256,4096]{1,0:T(8,128)(2,1)S(1)}, bf16[256,4096]{1,0:T(8,128)(2,1)}, u32[]{:S(2)}) %copy-start.5) | copy-done | bytes 2097176
  88.6 1.6 %copy-done.8 = bf16[256,4096]{1,0:T(8,128)(2,1)S(1)} copy-done((bf16[256,4096]{1,0:T(8,128)(2,1)S(1)}, bf16[256,4096]{1,0:T(8,128)(2,1)}, u32[]{:S(2)}) %copy-start.8) | copy-done | bytes 2097176
  90.2 1.0 shard_map.52
  91.3 1.0 shard_map.51
  92.4 1.5 collective-permute-start.4
  93.9 1.0 shard_map.50
  94.9 0.4 collective-permute-start.3
  95.3 1.0 shard_map.49.own_ref
  96.4 0.6 collective-permute-done.5.r3_ref
  97.0 1.9 %collective-permute-done.4.r2_ref = bf16[1024,128]{1,0:T(8,128)(2,1)S(1)} collective-permute-done((bf16[1024,128]{1,0:T(8,128)(2,1)S(1)}, bf16[1024,128]{1,0:T(8,128)(2,1)S(1)}, u32[]{:S(2)}, u32[]{:S(2)}) %collective-permute-start.4) | collective-permute-done | bytes 262176 | tf_op jit(solution)/shard_map/ppermute | solution.py:271
  98.9 4.4 %collective-permute-done.3.r1_ref = bf16[1024,128]{1,0:T(8,128)(2,1)S(1)} collective-permute-done((bf16[1024,128]{1,0:T(8,128)(2,1)S(1)}, bf16[1024,128]{1,0:T(8,128)(2,1)S(1)}, u32[]{:S(2)}, u32[]{:S(2)}) %collective-permute-start.3) | collective-permute-done | bytes 262176 | tf_op jit(solution)/shard_map/ppermute | solution.py:271
  103.3 1.4 shard_map.53
  104.6 6.4 %all-to-all-start = ((bf16[8,128,128]{2,1,0:T(8,128)(2,1)}), bf16[8,128,128]{2,1,0:T(8,128)(2,1)S(1)}, u32[]{:S(2)}, u32[]{:S(2)}) async-start(bf16[8,128,128]{2,1,0:T(8,128)(2,1)} %get-tuple-element.37), calls=%async_computation | async-start | bytes 524288 | tf_op jit(solution)/shard_map/all_to_all | solution.py:240
  111.0 0.9 copy-done.15
  111.9 0.6 shard_map.65
  112.6 1.6 %shard_map.59 = (f32[192,128]{1,0:T(8,128)S(1)}, f32[8,128]{1,0:T(8,128)S(1)}) custom-call(s32[4]{0:T(128)S(1)} %pad_add_fusion.at_ref, f32[1]{0:T(128)S(6)} %mul.3.weight_ref, f32[192,128]{1,0:T(8,128)S(1)} %copy-done.17, bf16[8,192,128]{2,1,0:T(8,128)(2,1)} %all-to-all-done.1.arrived_ref), custom_call_target="tpu_custom_call" | custom-call | flops 786432 | bytes 786432 | tf_op jit(solution)/shard_map/pallas_call | solution.py:167
  114.2 6.1 %all-to-all-done.arrived_ref = bf16[8,128,128]{2,1,0:T(8,128)(2,1)S(1)} async-done(((bf16[8,128,128]{2,1,0:T(8,128)(2,1)}), bf16[8,128,128]{2,1,0:T(8,128)(2,1)S(1)}, u32[]{:S(2)}, u32[]{:S(2)}) %all-to-all-start) | async-done | bytes 262176 | tf_op jit(solution)/shard_map/all_to_all | solution.py:240
  120.3 0.6 shard_map.66
  121.0 1.3 collective-permute-start.12
  122.3 2.6 %collective-permute-start.13 = (f32[128,128]{1,0:T(8,128)S(1)}, f32[128,128]{1,0:T(8,128)S(1)}, u32[]{:S(2)}, u32[]{:S(2)}) collective-permute-start(f32[128,128]{1,0:T(8,128)S(1)} %get-tuple-element.49), channel_id=1, source_target_pairs={{0,128},{64,192},{128,0},{192,64},{1,129},{65,193},{129,1},{193,65... | collective-permute-start | bytes 196616 | tf_op jit(solution)/shard_map/ppermute | solution.py:279
  125.0 1.1 collective-permute-start.14
  126.0 16.8 %all_to_all.25.in_ref = f32[16,1,128]{2,1,0:T(1,128)S(1)} all-to-all(f32[16,1,128]{2,1,0:T(1,128)S(1)} %get-tuple-element.46), channel_id=1, replica_groups=mesh['dp'=4,'x'=4,'z'=8,'core'=2] {'z','core'}, dimensions={0} | all-to-all | bytes 16384 | tf_op jit(solution)/shard_map/all_to_all | solution.py:240
  142.9 0.6 shard_map.67
  143.5 3.5 %all-to-all-start.4 = ((f32[16,1,128]{2,1,0:T(1,128)}), f32[16,1,128]{2,1,0:T(1,128)S(1)}, u32[]{:S(2)}, u32[]{:S(2)}) async-start(f32[16,1,128]{2,1,0:T(1,128)} %shard_map.67), calls=%async_computation.4 | async-start | bytes 16384 | tf_op jit(solution)/shard_map/all_to_all | solution.py:240
  147.1 6.1 %all-to-all-done.4.squares_ref = f32[16,1,128]{2,1,0:T(1,128)S(1)} async-done(((f32[16,1,128]{2,1,0:T(1,128)}), f32[16,1,128]{2,1,0:T(1,128)S(1)}, u32[]{:S(2)}, u32[]{:S(2)}) %all-to-all-start.4) | async-done | bytes 8224 | tf_op jit(solution)/shard_map/all_to_all | solution.py:240
  153.3 1.3 shard_map.70
  (37 shorter events, 0.9 us)
Async XLA Ops:
  0.7 3.4 %copy-start.9 = (bf16[1,512,8192]{2,1,0:T(8,128)(2,1)S(1)}, bf16[1,512,8192]{2,1,0:T(8,128)(2,1)}, u32[]{:S(2)}) copy-start(bf16[1,512,8192]{2,1,0:T(8,128)(2,1)} %param.4) | copy-start | bytes 25165828
  4.1 0.8 copy-start.13
  7.4 6.0 %copy-start.10 = (bf16[1,512,512]{2,1,0:T(8,128)(2,1)S(1)}, bf16[1,512,512]{2,1,0:T(8,128)(2,1)}, u32[]{:S(2)}) copy-start(bf16[1,512,512]{2,1,0:T(8,128)(2,1)} %param.6) | copy-start | bytes 1572868
  7.5 10.9 %collective-permute-start.1 = (bf16[256,4096]{1,0:T(8,128)(2,1)S(1)}, bf16[256,4096]{1,0:T(8,128)(2,1)S(1)}, u32[]{:S(2)}, u32[]{:S(2)}) collective-permute-start(bf16[256,4096]{1,0:T(8,128)(2,1)S(1)} %get-tuple-element.35), channel_id=1, source_target_pairs={{0,1},{1,0},{2,3},{3,2},{4,5},{5,4},{6,7},{7,6},{8,9},{9,8},{10,11... | collective-permute-start | bytes 6291464 | tf_op jit(solution)/shard_map/ppermute | solution.py:257
  13.3 11.2 %copy-start.3 = (bf16[256,4096]{1,0:T(8,128)(2,1)}, bf16[256,4096]{1,0:T(8,128)(2,1)S(1)}, u32[]{:S(2)}) copy-start(bf16[256,4096]{1,0:T(8,128)(2,1)S(1)} %get-tuple-element.32.refs_0_) | copy-start | bytes 6291460
  13.3 5.0 %collective-permute-start = (bf16[256,4096]{1,0:T(8,128)(2,1)S(1)}, bf16[256,4096]{1,0:T(8,128)(2,1)S(1)}, u32[]{:S(2)}, u32[]{:S(2)}) collective-permute-start(bf16[256,4096]{1,0:T(8,128)(2,1)S(1)} %get-tuple-element.34), channel_id=1, source_target_pairs={{0,1},{1,0},{2,3},{3,2},{4,5},{5,4},{6,7},{7,6},{8,9},{9,8},{10,11... | collective-permute-start | bytes 6291464 | tf_op jit(solution)/shard_map/ppermute | solution.py:257
  13.6 4.7 %collective-permute-start.2 = (bf16[512,512]{1,0:T(8,128)(2,1)S(1)}, bf16[512,512]{1,0:T(8,128)(2,1)S(1)}, u32[]{:S(2)}, u32[]{:S(2)}) collective-permute-start(bf16[512,512]{1,0:T(8,128)(2,1)S(1)} %shard_map.48.refs_4_), channel_id=1, source_target_pairs={{0,1},{1,0},{2,3},{3,2},{4,5},{5,4},{6,7},{7,6},{8,9},{9,8},{10,11... | collective-permute-start | bytes 1572872 | tf_op jit(solution)/shard_map/ppermute | solution.py:260
  18.3 6.2 %copy-start = (bf16[256,4096]{1,0:T(8,128)(2,1)}, bf16[256,4096]{1,0:T(8,128)(2,1)S(1)}, u32[]{:S(2)}) copy-start(bf16[256,4096]{1,0:T(8,128)(2,1)S(1)} %collective-permute-done.1.refs_3_) | copy-start | bytes 6291460
  18.3 6.2 %copy-start.6 = (bf16[256,4096]{1,0:T(8,128)(2,1)}, bf16[256,4096]{1,0:T(8,128)(2,1)S(1)}, u32[]{:S(2)}) copy-start(bf16[256,4096]{1,0:T(8,128)(2,1)S(1)} %collective-permute-done.refs_2_) | copy-start | bytes 6291460
  19.5 10.4 %collective-permute-start.11 = (bf16[1536,128]{1,0:T(8,128)(2,1)S(1)}, bf16[1536,128]{1,0:T(8,128)(2,1)S(1)}, u32[]{:S(2)}, u32[]{:S(2)}) collective-permute-start(bf16[1536,128]{1,0:T(8,128)(2,1)S(1)} %shard_map.63), channel_id=1, source_target_pairs={{0,48},{16,0},{32,16},{48,32},{1,49},{17,1},{33,17},{49,33},{2,50}... | collective-permute-start | bytes 1179656 | tf_op jit(solution)/shard_map/ppermute | solution.py:271
  21.5 12.3 %collective-permute-start.10 = (bf16[1536,128]{1,0:T(8,128)(2,1)S(1)}, bf16[1536,128]{1,0:T(8,128)(2,1)S(1)}, u32[]{:S(2)}, u32[]{:S(2)}) collective-permute-start(bf16[1536,128]{1,0:T(8,128)(2,1)S(1)} %shard_map.62), channel_id=1, source_target_pairs={{0,16},{16,32},{32,48},{48,0},{1,17},{17,33},{33,49},{49,1},{2,18}... | collective-permute-start | bytes 1179656 | tf_op jit(solution)/shard_map/ppermute | solution.py:271
  23.4 17.0 %collective-permute-start.9 = (bf16[1536,128]{1,0:T(8,128)(2,1)S(1)}, bf16[1536,128]{1,0:T(8,128)(2,1)S(1)}, u32[]{:S(2)}, u32[]{:S(2)}) collective-permute-start(bf16[1536,128]{1,0:T(8,128)(2,1)S(1)} %shard_map.61), channel_id=1, source_target_pairs={{0,32},{16,48},{32,0},{48,16},{1,33},{17,49},{33,1},{49,17},{2,34}... | collective-permute-start | bytes 1179656 | tf_op jit(solution)/shard_map/ppermute | solution.py:271
  41.1 0.8 copy-start.12
  41.9 0.6 copy-start.14
  42.5 36.6 %all-to-all-start.2 = ((bf16[8,192,128]{2,1,0:T(8,128)(2,1)}), bf16[8,192,128]{2,1,0:T(8,128)(2,1)S(1)}, u32[]{:S(2)}, u32[]{:S(2)}) async-start(bf16[8,192,128]{2,1,0:T(8,128)(2,1)} %copy-done.12), calls=%async_computation.2 | async-start | bytes 786432 | tf_op jit(solution)/shard_map/all_to_all | solution.py:240
  50.7 1.6 %copy-start.1 = (bf16[256,4096]{1,0:T(8,128)(2,1)S(1)}, bf16[256,4096]{1,0:T(8,128)(2,1)}, u32[]{:S(2)}) copy-start(bf16[256,4096]{1,0:T(8,128)(2,1)} %copy-done) | copy-start | bytes 6291460
  52.3 1.6 %copy-start.4 = (bf16[256,4096]{1,0:T(8,128)(2,1)S(1)}, bf16[256,4096]{1,0:T(8,128)(2,1)}, u32[]{:S(2)}) copy-start(bf16[256,4096]{1,0:T(8,128)(2,1)} %copy-done.3) | copy-start | bytes 6291460
  53.9 1.6 %copy-start.7 = (bf16[256,4096]{1,0:T(8,128)(2,1)S(1)}, bf16[256,4096]{1,0:T(8,128)(2,1)}, u32[]{:S(2)}) copy-start(bf16[256,4096]{1,0:T(8,128)(2,1)} %copy-done.6) | copy-start | bytes 6291460
  56.6 8.3 %collective-permute-start.8 = (bf16[1536,128]{1,0:T(8,128)(2,1)S(1)}, bf16[1536,128]{1,0:T(8,128)(2,1)S(1)}, u32[]{:S(2)}, u32[]{:S(2)}) collective-permute-start(bf16[1536,128]{1,0:T(8,128)(2,1)S(1)} %shard_map.57), channel_id=1, source_target_pairs={{0,48},{16,0},{32,16},{48,32},{1,49},{17,1},{33,17},{49,33},{2,50}... | collective-permute-start | bytes 1179656 | tf_op jit(solution)/shard_map/ppermute | solution.py:271
  58.0 9.3 %collective-permute-start.7 = (bf16[1536,128]{1,0:T(8,128)(2,1)S(1)}, bf16[1536,128]{1,0:T(8,128)(2,1)S(1)}, u32[]{:S(2)}, u32[]{:S(2)}) collective-permute-start(bf16[1536,128]{1,0:T(8,128)(2,1)S(1)} %shard_map.56), channel_id=1, source_target_pairs={{0,16},{16,32},{32,48},{48,0},{1,17},{17,33},{33,49},{49,1},{2,18}... | collective-permute-start | bytes 1179656 | tf_op jit(solution)/shard_map/ppermute | solution.py:271
  60.7 16.2 %collective-permute-start.6 = (bf16[1536,128]{1,0:T(8,128)(2,1)S(1)}, bf16[1536,128]{1,0:T(8,128)(2,1)S(1)}, u32[]{:S(2)}, u32[]{:S(2)}) collective-permute-start(bf16[1536,128]{1,0:T(8,128)(2,1)S(1)} %shard_map.55), channel_id=1, source_target_pairs={{0,32},{16,48},{32,0},{48,16},{1,33},{17,49},{33,1},{49,17},{2,34}... | collective-permute-start | bytes 1179656 | tf_op jit(solution)/shard_map/ppermute | solution.py:271
  77.7 0.7 copy-start.11
  78.4 0.6 copy-start.16
  79.1 25.6 %all-to-all-start.1 = ((bf16[8,192,128]{2,1,0:T(8,128)(2,1)}), bf16[8,192,128]{2,1,0:T(8,128)(2,1)}, u32[]{:S(2)}, u32[]{:S(2)}) async-start(bf16[8,192,128]{2,1,0:T(8,128)(2,1)} %copy-done.11), calls=%async_computation.1 | async-start | bytes 786432 | tf_op jit(solution)/shard_map/all_to_all | solution.py:240
  85.5 1.6 %copy-start.2 = (bf16[256,4096]{1,0:T(8,128)(2,1)S(1)}, bf16[256,4096]{1,0:T(8,128)(2,1)}, u32[]{:S(2)}) copy-start(bf16[256,4096]{1,0:T(8,128)(2,1)} %copy-done) | copy-start | bytes 6291460
  87.0 1.6 %copy-start.5 = (bf16[256,4096]{1,0:T(8,128)(2,1)S(1)}, bf16[256,4096]{1,0:T(8,128)(2,1)}, u32[]{:S(2)}) copy-start(bf16[256,4096]{1,0:T(8,128)(2,1)} %copy-done.3) | copy-start | bytes 6291460
  88.6 1.6 %copy-start.8 = (bf16[256,4096]{1,0:T(8,128)(2,1)S(1)}, bf16[256,4096]{1,0:T(8,128)(2,1)}, u32[]{:S(2)}) copy-start(bf16[256,4096]{1,0:T(8,128)(2,1)} %copy-done.6) | copy-start | bytes 6291460
  91.3 5.7 %collective-permute-start.5 = (bf16[1024,128]{1,0:T(8,128)(2,1)S(1)}, bf16[1024,128]{1,0:T(8,128)(2,1)S(1)}, u32[]{:S(2)}, u32[]{:S(2)}) collective-permute-start(bf16[1024,128]{1,0:T(8,128)(2,1)S(1)} %shard_map.52), channel_id=1, source_target_pairs={{0,48},{16,0},{32,16},{48,32},{1,49},{17,1},{33,17},{49,33},{2,50}... | collective-permute-start | bytes 786440 | tf_op jit(solution)/shard_map/ppermute | solution.py:271
  92.4 6.5 %collective-permute-start.4 = (bf16[1024,128]{1,0:T(8,128)(2,1)S(1)}, bf16[1024,128]{1,0:T(8,128)(2,1)S(1)}, u32[]{:S(2)}, u32[]{:S(2)}) collective-permute-start(bf16[1024,128]{1,0:T(8,128)(2,1)S(1)} %shard_map.51), channel_id=1, source_target_pairs={{0,16},{16,32},{32,48},{48,0},{1,17},{17,33},{33,49},{49,1},{2,18}... | collective-permute-start | bytes 786440 | tf_op jit(solution)/shard_map/ppermute | solution.py:271
  94.9 8.3 %collective-permute-start.3 = (bf16[1024,128]{1,0:T(8,128)(2,1)S(1)}, bf16[1024,128]{1,0:T(8,128)(2,1)S(1)}, u32[]{:S(2)}, u32[]{:S(2)}) collective-permute-start(bf16[1024,128]{1,0:T(8,128)(2,1)S(1)} %shard_map.50), channel_id=1, source_target_pairs={{0,32},{16,48},{32,0},{48,16},{1,33},{17,49},{33,1},{49,17},{2,34}... | collective-permute-start | bytes 786440 | tf_op jit(solution)/shard_map/ppermute | solution.py:271
  96.4 16.2 %copy-start.17 = (f32[192,128]{1,0:T(8,128)S(1)}, f32[192,128]{1,0:T(8,128)}, u32[]{:S(2)}) copy-start(f32[192,128]{1,0:T(8,128)} %copy-done.16) | copy-start | bytes 294916
  104.6 15.7 %all-to-all-start = ((bf16[8,128,128]{2,1,0:T(8,128)(2,1)}), bf16[8,128,128]{2,1,0:T(8,128)(2,1)S(1)}, u32[]{:S(2)}, u32[]{:S(2)}) async-start(bf16[8,128,128]{2,1,0:T(8,128)(2,1)} %get-tuple-element.37), calls=%async_computation | async-start | bytes 524288 | tf_op jit(solution)/shard_map/all_to_all | solution.py:240
  111.0 0.9 copy-start.15
  121.0 26.0 %collective-permute-start.12 = (f32[128,128]{1,0:T(8,128)S(1)}, f32[128,128]{1,0:T(8,128)S(1)}, u32[]{:S(2)}, u32[]{:S(2)}) collective-permute-start(f32[128,128]{1,0:T(8,128)S(1)} %get-tuple-element.48), channel_id=1, source_target_pairs={{0,64},{64,128},{128,192},{192,0},{1,65},{65,129},{129,193},{193,1... | collective-permute-start | bytes 196616 | tf_op jit(solution)/shard_map/ppermute | solution.py:279
  122.3 24.7 %collective-permute-start.13 = (f32[128,128]{1,0:T(8,128)S(1)}, f32[128,128]{1,0:T(8,128)S(1)}, u32[]{:S(2)}, u32[]{:S(2)}) collective-permute-start(f32[128,128]{1,0:T(8,128)S(1)} %get-tuple-element.49), channel_id=1, source_target_pairs={{0,128},{64,192},{128,0},{192,64},{1,129},{65,193},{129,1},{193,65... | collective-permute-start | bytes 196616 | tf_op jit(solution)/shard_map/ppermute | solution.py:279
  125.0 22.0 %collective-permute-start.14 = (f32[128,128]{1,0:T(8,128)S(1)}, f32[128,128]{1,0:T(8,128)S(1)}, u32[]{:S(2)}, u32[]{:S(2)}) collective-permute-start(f32[128,128]{1,0:T(8,128)S(1)} %get-tuple-element.50), channel_id=1, source_target_pairs={{0,192},{64,0},{128,64},{192,128},{1,193},{65,1},{129,65},{193,129... | collective-permute-start | bytes 196616 | tf_op jit(solution)/shard_map/ppermute | solution.py:279
  143.5 9.8 %all-to-all-start.4 = ((f32[16,1,128]{2,1,0:T(1,128)}), f32[16,1,128]{2,1,0:T(1,128)S(1)}, u32[]{:S(2)}, u32[]{:S(2)}) async-start(f32[16,1,128]{2,1,0:T(1,128)} %shard_map.67), calls=%async_computation.4 | async-start | bytes 16384 | tf_op jit(solution)/shard_map/all_to_all | solution.py:240
